TPU v7x, 8 devices: a whole 2x2x1 slice. The times are simulated.
8 devices in a mesh: part: 1 (over z), row: 2 (over y), col: 4 (over x, core).
Axes of the slice: x: 2, y: 2, z: 1, core: 2. Of those that a mesh axis runs over, the one named last changes fastest.
Arguments:
- counts: bfloat16 [8192, 16384], P(('part', 'row'), 'col')
- w_init: float32 [8192, 768], P(('part', 'row'))
- h_init: float32 [768, 16384], P(None, ('part', 'col'))
Outputs:
- output 1: float32 [8192, 768], P(('part', 'row'))
- output 2: float32 [768, 16384], P(None, ('part', 'col'))
All inputs are finite; a program needn't handle non-finite values.
Results may differ from a plain program's by a relative error of at most 0.001.
Values are sent between devices in bfloat16 or wider.
A program may use at most 1 GiB of HBM per device.

v0:
```python
import jax
import jax.numpy as jnp
from jax import lax
from jax.sharding import PartitionSpec as P

SWEEPS = 4
EPS = 1e-6
CONTRACT_WORDS = (((1,), (1,)), ((), ()))
CONTRACT_DOCS = (((0,), (0,)), ((), ()))


def ratio_block(c_blk, w_bf, h_bf):
    z_blk = jnp.dot(w_bf, h_bf, preferred_element_type=jnp.float32)
    return (c_blk.astype(jnp.float32) / (z_blk + EPS)).astype(jnp.bfloat16)


def local_sweeps(c_blk, w_loc, h_loc):
    for sweep_index in range(SWEEPS):
        h_bf = h_loc.astype(jnp.bfloat16)
        q_blk = ratio_block(c_blk, w_loc.astype(jnp.bfloat16), h_bf)
        a_w = lax.psum(lax.dot_general(q_blk, h_bf, CONTRACT_WORDS, preferred_element_type=jnp.float32), 'col')
        s_h = lax.psum(jnp.sum(h_loc, axis=1), 'col')
        w_loc = w_loc * a_w / s_h
        w_bf = w_loc.astype(jnp.bfloat16)
        q_blk = ratio_block(c_blk, w_bf, h_bf)
        a_h = lax.psum(lax.dot_general(w_bf, q_blk, CONTRACT_DOCS, preferred_element_type=jnp.float32), 'row')
        s_w = lax.psum(jnp.sum(w_loc, axis=0), 'row')
        h_loc = h_loc * a_h / s_w[:, None]
    return w_loc, h_loc


def solution(mesh):
    spec_c = P(('part', 'row'), 'col')
    spec_w = P(('part', 'row'), None)
    spec_h = P(None, ('part', 'col'))
    return jax.shard_map(local_sweeps, mesh=mesh, in_specs=(spec_c, spec_w, spec_h), out_specs=(spec_w, spec_h), check_vma=False)
```

profile of v0, /device:TPU:1, one launch (start us, length us, event | category | flops | bytes accessed | tf_op | source)
XLA Modules:
  0.0 2714.4 jit_solution(2633494495537376656)
XLA Ops:
  7.2 0.0 all-reduce.9.cloned.1.call-start
  7.2 38.6 %fusion.clone.5 = bf16[4096,4096]{1,0:T(8,128)(2,1)} fusion(bf16[4096,4096]{1,0:T(8,128)(2,1)} %param.3, f32[4096,768]{1,0:T(8,128)} %param.4, f32[768,4096]{1,0:T(8,128)} %param.5), kind=kOutput, calls=%fused_computation.8.clone.clone.clone.2 | convolution fusion | flops 25843204096 | bytes 92274688 | tf_op jit(solution)/shard_map/dot_general | solution.py:13
  45.8 35.4 %fusion.11 = f32[4096,768]{1,0:T(8,128)} fusion(f32[768,4096]{1,0:T(8,128)} %param.5, bf16[4096,4096]{1,0:T(8,128)(2,1)} %fusion.clone.5), kind=kOutput, calls=%fused_computation.19 | convolution fusion | flops 25772949504 | bytes 58720256 | tf_op jit(solution)/shard_map/dot_general | solution.py:21
  81.2 0.0 all-reduce.9.cloned.1.call-update
  81.2 0.0 all-reduce.11.cloned.1.call-start
  81.3 5.2 reduce_sum.72
  86.5 6.9 psum.113
  93.4 204.3 %all-reduce.9.cloned.1.call-done = f32[4096,768]{1,0:T(8,128)} async-done(((f32[4096,768]{1,0:T(8,128)}), f32[4096,768]{1,0:T(8,128)}) %all-reduce.9.cloned.1.call-update) | async-done | bytes 12582928 | tf_op jit(solution)/shard_map/psum | solution.py:21
  297.7 14.1 fusion.62
  311.8 38.6 %fusion.1.clone.2 = bf16[4096,4096]{1,0:T(8,128)(2,1)} fusion(bf16[4096,4096]{1,0:T(8,128)(2,1)} %param.3, f32[4096,768]{1,0:T(8,128)} %get-tuple-element.15, f32[768,4096]{1,0:T(8,128)} %param.5), kind=kOutput, calls=%fused_computation.9.clone.clone.clone | convolution fusion | flops 25843204096 | bytes 92274688 | tf_op jit(solution)/shard_map/dot_general | solution.py:13
  350.4 35.6 %fusion.15 = f32[768,4096]{1,0:T(8,128)} fusion(f32[4096,768]{1,0:T(8,128)} %get-tuple-element.15, bf16[4096,4096]{1,0:T(8,128)(2,1)} %fusion.1.clone.2), kind=kOutput, calls=%fused_computation.23 | convolution fusion | flops 25772949504 | bytes 58720256 | tf_op jit(solution)/shard_map/dot_general | solution.py:26
  386.0 0.0 all-reduce.11.cloned.1.call-update
  386.0 0.0 all-reduce.13.cloned.1.call-start
  386.1 3.9 psum.115
  390.0 278.9 %all-reduce.11.cloned.1.call-done = f32[768,4096]{1,0:T(8,128)} async-done(((f32[768,4096]{1,0:T(8,128)}), f32[768,4096]{1,0:T(8,128)}) %all-reduce.11.cloned.1.call-update) | async-done | bytes 12582928 | tf_op jit(solution)/shard_map/psum | solution.py:26
  668.9 14.5 fusion.61
  683.4 38.6 %fusion.2.clone.2 = bf16[4096,4096]{1,0:T(8,128)(2,1)} fusion(bf16[4096,4096]{1,0:T(8,128)(2,1)} %param.3, f32[768,4096]{1,0:T(8,128)} %get-tuple-element.13, f32[4096,768]{1,0:T(8,128)} %get-tuple-element.15), kind=kOutput, calls=%fused_computation.10.clone.clone.clone | convolution fusion | flops 25843204096 | bytes 92274688 | tf_op jit(solution)/shard_map/dot_general | solution.py:13
  722.0 35.3 %fusion.10 = f32[4096,768]{1,0:T(8,128)} fusion(f32[768,4096]{1,0:T(8,128)} %get-tuple-element.13, bf16[4096,4096]{1,0:T(8,128)(2,1)} %fusion.2.clone.2), kind=kOutput, calls=%fused_computation.18 | convolution fusion | flops 25772949504 | bytes 58720256 | tf_op jit(solution)/shard_map/dot_general | solution.py:21
  757.4 0.0 copy-start.2
  757.4 0.0 all-reduce.13.cloned.1.call-update
  757.4 0.0 all-reduce.15.cloned.1.call-start
  757.4 0.6 copy-done.2
  758.0 6.2 psum.117
  764.2 208.1 %all-reduce.13.cloned.1.call-done = f32[4096,768]{1,0:T(8,128)} async-done(((f32[4096,768]{1,0:T(8,128)}), f32[4096,768]{1,0:T(8,128)}) %all-reduce.13.cloned.1.call-update) | async-done | bytes 12582928 | tf_op jit(solution)/shard_map/psum | solution.py:21
  972.3 14.1 fusion.60
  986.4 38.6 %fusion.3.clone.2 = bf16[4096,4096]{1,0:T(8,128)(2,1)} fusion(bf16[4096,4096]{1,0:T(8,128)(2,1)} %param.3, f32[4096,768]{1,0:T(8,128)} %get-tuple-element.11, f32[768,4096]{1,0:T(8,128)} %get-tuple-element.13), kind=kOutput, calls=%fused_computation.11.clone.clone.clone | convolution fusion | flops 25843204096 | bytes 92274688 | tf_op jit(solution)/shard_map/dot_general | solution.py:13
  1024.9 35.6 %fusion.14 = f32[768,4096]{1,0:T(8,128)} fusion(f32[4096,768]{1,0:T(8,128)} %get-tuple-element.11, bf16[4096,4096]{1,0:T(8,128)(2,1)} %fusion.3.clone.2), kind=kOutput, calls=%fused_computation.22 | convolution fusion | flops 25772949504 | bytes 58720256 | tf_op jit(solution)/shard_map/dot_general | solution.py:26
  1060.6 0.0 all-reduce.15.cloned.1.call-update
  1060.6 0.0 all-reduce.17.cloned.1.call-start
  1060.7 4.2 psum.119
  1064.8 278.6 %all-reduce.15.cloned.1.call-done = f32[768,4096]{1,0:T(8,128)} async-done(((f32[768,4096]{1,0:T(8,128)}), f32[768,4096]{1,0:T(8,128)}) %all-reduce.15.cloned.1.call-update) | async-done | bytes 12582928 | tf_op jit(solution)/shard_map/psum | solution.py:26
  1343.5 14.5 fusion.59
  1358.0 38.6 %fusion.4.clone.2 = bf16[4096,4096]{1,0:T(8,128)(2,1)} fusion(bf16[4096,4096]{1,0:T(8,128)(2,1)} %param.3, f32[768,4096]{1,0:T(8,128)} %get-tuple-element.9, f32[4096,768]{1,0:T(8,128)} %get-tuple-element.11), kind=kOutput, calls=%fused_computation.12.clone.clone.clone | convolution fusion | flops 25843204096 | bytes 92274688 | tf_op jit(solution)/shard_map/dot_general | solution.py:13
  1396.6 35.3 %fusion.9 = f32[4096,768]{1,0:T(8,128)} fusion(f32[768,4096]{1,0:T(8,128)} %get-tuple-element.9, bf16[4096,4096]{1,0:T(8,128)(2,1)} %fusion.4.clone.2), kind=kOutput, calls=%fused_computation.17 | convolution fusion | flops 25772949504 | bytes 58720256 | tf_op jit(solution)/shard_map/dot_general | solution.py:21
  1431.9 0.0 copy-start
  1431.9 0.0 all-reduce.17.cloned.1.call-update
  1431.9 0.0 all-reduce.19.cloned.1.call-start
  1432.0 0.6 copy-done
  1432.6 6.1 psum.121
  1438.7 208.1 %all-reduce.17.cloned.1.call-done = f32[4096,768]{1,0:T(8,128)} async-done(((f32[4096,768]{1,0:T(8,128)}), f32[4096,768]{1,0:T(8,128)}) %all-reduce.17.cloned.1.call-update) | async-done | bytes 12582928 | tf_op jit(solution)/shard_map/psum | solution.py:21
  1646.9 14.1 fusion.58
  1660.9 38.6 %fusion.5.clone.2 = bf16[4096,4096]{1,0:T(8,128)(2,1)} fusion(bf16[4096,4096]{1,0:T(8,128)(2,1)} %param.3, f32[4096,768]{1,0:T(8,128)} %get-tuple-element.7, f32[768,4096]{1,0:T(8,128)} %get-tuple-element.9), kind=kOutput, calls=%fused_computation.13.clone.clone.clone | convolution fusion | flops 25843204096 | bytes 92274688 | tf_op jit(solution)/shard_map/dot_general | solution.py:13
  1699.5 35.6 %fusion.13 = f32[768,4096]{1,0:T(8,128)} fusion(f32[4096,768]{1,0:T(8,128)} %get-tuple-element.7, bf16[4096,4096]{1,0:T(8,128)(2,1)} %fusion.5.clone.2), kind=kOutput, calls=%fused_computation.21 | convolution fusion | flops 25772949504 | bytes 58720256 | tf_op jit(solution)/shard_map/dot_general | solution.py:26
  1735.1 0.0 all-reduce.19.cloned.1.call-update
  1735.2 0.0 all-reduce.21.cloned.1.call-start
  1735.2 4.0 psum.123
  1739.2 278.8 %all-reduce.19.cloned.1.call-done = f32[768,4096]{1,0:T(8,128)} async-done(((f32[768,4096]{1,0:T(8,128)}), f32[768,4096]{1,0:T(8,128)}) %all-reduce.19.cloned.1.call-update) | async-done | bytes 12582928 | tf_op jit(solution)/shard_map/psum | solution.py:26
  2018.0 14.4 fusion.57
  2032.5 38.6 %fusion.6.clone.5 = bf16[4096,4096]{1,0:T(8,128)(2,1)} fusion(bf16[4096,4096]{1,0:T(8,128)(2,1)} %param.3, f32[768,4096]{1,0:T(8,128)} %get-tuple-element.5, f32[4096,768]{1,0:T(8,128)} %get-tuple-element.7), kind=kOutput, calls=%fused_computation.14.clone.clone.clone.2 | convolution fusion | flops 25843204096 | bytes 92274688 | tf_op jit(solution)/shard_map/dot_general | solution.py:13
  2071.0 35.4 %fusion.8 = f32[4096,768]{1,0:T(8,128)} fusion(f32[768,4096]{1,0:T(8,128)} %get-tuple-element.5, bf16[4096,4096]{1,0:T(8,128)(2,1)} %fusion.6.clone.5), kind=kOutput, calls=%fused_computation.16 | convolution fusion | flops 25772949504 | bytes 58720256 | tf_op jit(solution)/shard_map/dot_general | solution.py:21
  2106.4 0.0 copy-start.1
  2106.4 0.0 all-reduce.21.cloned.1.call-update
  2106.5 0.0 all-reduce.23.cloned.1.call-start
  2106.5 0.6 copy-done.1
  2107.1 6.2 psum.125
  2113.3 208.0 %all-reduce.21.cloned.1.call-done = f32[4096,768]{1,0:T(8,128)} async-done(((f32[4096,768]{1,0:T(8,128)}), f32[4096,768]{1,0:T(8,128)}) %all-reduce.21.cloned.1.call-update) | async-done | bytes 12582928 | tf_op jit(solution)/shard_map/psum | solution.py:21
  2321.4 14.1 fusion.56
  2335.4 38.6 %fusion.7.clone.5 = bf16[4096,4096]{1,0:T(8,128)(2,1)} fusion(bf16[4096,4096]{1,0:T(8,128)(2,1)} %param.3, f32[4096,768]{1,0:T(8,128)} %get-tuple-element.3, f32[768,4096]{1,0:T(8,128)} %get-tuple-element.5), kind=kOutput, calls=%fused_computation.15.clone.clone.clone.2 | convolution fusion | flops 25843204096 | bytes 92274688 | tf_op jit(solution)/shard_map/dot_general | solution.py:13
  2374.0 35.6 %fusion.12 = f32[768,4096]{1,0:T(8,128)} fusion(f32[4096,768]{1,0:T(8,128)} %get-tuple-element.3, bf16[4096,4096]{1,0:T(8,128)(2,1)} %fusion.7.clone.5), kind=kOutput, calls=%fused_computation.20 | convolution fusion | flops 25772949504 | bytes 58720256 | tf_op jit(solution)/shard_map/dot_general | solution.py:26
  2409.7 0.0 all-reduce.23.cloned.1.call-update
  2409.7 3.8 psum.127
  2413.5 279.1 %all-reduce.23.cloned.1.call-done = f32[768,4096]{1,0:T(8,128)} async-done(((f32[768,4096]{1,0:T(8,128)}), f32[768,4096]{1,0:T(8,128)}) %all-reduce.23.cloned.1.call-update) | async-done | bytes 12582928 | tf_op jit(solution)/shard_map/psum | solution.py:26
  2692.5 14.5 multiply_divide_fusion
Async XLA Ops:
  7.2 290.6 %all-reduce.9.cloned.1.call-start = ((), (), s32[]{:S(2)}) async-start(), calls=%async_computation | async-start | bytes 25165824 | tf_op jit(solution)/shard_map/psum | solution.py:21
  81.2 587.6 %all-reduce.11.cloned.1.call-start = ((), (), s32[]{:S(2)}) async-start(), calls=%async_computation.1 | async-start | bytes 25165824 | tf_op jit(solution)/shard_map/psum | solution.py:26
  386.0 586.3 %all-reduce.13.cloned.1.call-start = ((), (), s32[]{:S(2)}) async-start(), calls=%async_computation.2 | async-start | bytes 25165824 | tf_op jit(solution)/shard_map/psum | solution.py:21
  757.4 0.7 copy-start.2
  757.4 586.1 %all-reduce.15.cloned.1.call-start = ((), (), s32[]{:S(2)}) async-start(), calls=%async_computation.3 | async-start | bytes 25165824 | tf_op jit(solution)/shard_map/psum | solution.py:26
  1060.6 586.3 %all-reduce.17.cloned.1.call-start = ((), (), s32[]{:S(2)}) async-start(), calls=%async_computation.4 | async-start | bytes 25165824 | tf_op jit(solution)/shard_map/psum | solution.py:21
  1431.9 0.7 copy-start
  1431.9 586.1 %all-reduce.19.cloned.1.call-start = ((), (), s32[]{:S(2)}) async-start(), calls=%async_computation.5 | async-start | bytes 25165824 | tf_op jit(solution)/shard_map/psum | solution.py:26
  1735.2 586.2 %all-reduce.21.cloned.1.call-start = ((), (), s32[]{:S(2)}) async-start(), calls=%async_computation.6 | async-start | bytes 25165824 | tf_op jit(solution)/shard_map/psum | solution.py:21
  2106.4 0.7 copy-start.1
  2106.5 586.1 %all-reduce.23.cloned.1.call-start = ((), (), s32[]{:S(2)}) async-start(), calls=%async_computation.7 | async-start | bytes 25165824 | tf_op jit(solution)/shard_map/psum | solution.py:26
Sparse Core Ops, SparseCore 0:
  81.4 216.3 all-reduce.8
  386.2 282.6 all-reduce.10
  757.5 214.7 all-reduce.12
  1060.7 282.6 all-reduce.14
  1432.1 214.7 all-reduce.16
  1735.3 282.6 all-reduce.18
  2106.6 214.7 all-reduce.20
  2409.8 282.6 all-reduce.22
where the time goes:
time: 2720 us; the launch traced here: 2710 us
  waiting for transfers between devices  1940 us (71%)
  matrix products  593 us (22%)
  other arithmetic  120 us (4%)
  blocking collectives  41.3 us (2%)
    psum x4, waiting for transfers between devices, local_sweeps(): lax.psum(lax.dot_general(w_bf, q_blk, CONTRACT_DOCS, preferred_element_ty...  1120 us
    psum x4, waiting for transfers between devices, local_sweeps(): lax.psum(lax.dot_general(q_blk, h_bf, CONTRACT_WORDS, preferred_element_t...  829 us
    dot_general x8, matrix products, ratio_block(): z_blk = jnp.dot(w_bf, h_bf, preferred_element_type=jnp.float32)  309 us
    dot_general x4, matrix products, local_sweeps(): lax.dot_general(w_bf, q_blk, CONTRACT_DOCS, preferred_element_type=jnp.fl...  143 us
    dot_general x4, matrix products, local_sweeps(): lax.dot_general(q_blk, h_bf, CONTRACT_WORDS, preferred_element_type=jnp.f...  142 us
    reduce_sum x4, other arithmetic, local_sweeps(): s_w = lax.psum(jnp.sum(w_loc, axis=0), 'row')  56.3 us
  transfers between devices with their start and end apart: 8, of which 8 were waited for; matrix products, arithmetic and copies ran while one was open for 0% of the time, Pallas kernels for 0%

commit v1 on v0

v1 whole, which is shorter than its diff:
```python
import functools

import jax
import jax.numpy as jnp
from jax import lax
from jax.experimental import pallas as pl
from jax.experimental.pallas import tpu as pltpu
from jax.sharding import Mesh, PartitionSpec as P

SWEEPS = 4
EPS = 1e-6
CHUNKS = 4
F32 = jnp.float32
BF16 = jnp.bfloat16
MIB = 2 ** 20
ALL = ('y', 'x', 'c')
MESH = pl.DeviceIdType.MESH
CONTRACT_WORDS = (((1,), (1,)), ((), ()))
CONTRACT_DOCS = (((0,), (0,)), ((), ()))


def ratio(c_tile, z_tile):
    return (c_tile.astype(F32) / (z_tile + EPS)).astype(BF16)


def w_kernel(tile, idx_ref, c_ref, w_ref, ho_ref, hs_ref, ka_ref, sa_ref, kb_ref, sb_ref, acc_ref):
    step = pl.program_id(0)
    words = c_ref.shape[1]
    half = w_ref.shape[0] // 2
    for t in range(words // tile):
        cols = pl.ds(t * tile, tile)
        h = jnp.concatenate([ho_ref[:, cols], hs_ref[:, cols]], axis=0)
        z = jnp.dot(w_ref[...], h, preferred_element_type=F32)
        q = ratio(c_ref[:, cols], z)
        part = lax.dot_general(q, h, CONTRACT_WORDS, preferred_element_type=F32)
        if t == 0:
            acc_ref[...] = part
        else:
            acc_ref[...] += part

    @pl.when(step < 2)
    def _():
        sa_ref[0] = acc_ref[:half]

    @pl.when(step >= 2)
    def _():
        ka_ref[0] = acc_ref[:half]

    @pl.when(step % 2 == 0)
    def _():
        sb_ref[0] = acc_ref[half:]

    @pl.when(step % 2 == 1)
    def _():
        kb_ref[0] = acc_ref[half:]


def w_partial(rows, c, w, h_own, h_sib, base):
    words, topics = c.shape[1], w.shape[1]
    idx = jnp.stack([rows[0] + base[0], rows[1] + base[0], rows[2] + base[0], rows[3] + base[0],
                     rows[0] + base[1], rows[1] + base[1], rows[2] + base[1], rows[3] + base[1]])
    part = jax.ShapeDtypeStruct((2, 128, topics), F32)
    block = (1, 128, topics)
    flops = 4 * 1024 * words * topics
    return pl.pallas_call(
        functools.partial(w_kernel, 1024),
        out_shape=(part,) * 4,
        grid_spec=pltpu.PrefetchScalarGridSpec(
            num_scalar_prefetch=1,
            grid=(4,),
            in_specs=[
                pl.BlockSpec((256, words), lambda i, s: (s[i], 0)),
                pl.BlockSpec((256, topics), lambda i, s: (s[4 + i], 0)),
                pl.BlockSpec((topics // 2, words), lambda i, s: (0, 0)),
                pl.BlockSpec((topics // 2, words), lambda i, s: (0, 0)),
            ],
            out_specs=[
                pl.BlockSpec(block, lambda i, s: (i // 3, 0, 0)),
                pl.BlockSpec(block, lambda i, s: (jnp.minimum(i, 1), 0, 0)),
                pl.BlockSpec(block, lambda i, s: (i // 2, 0, 0)),
                pl.BlockSpec(block, lambda i, s: (i // 2, 0, 0)),
            ],
            scratch_shapes=[pltpu.VMEM((256, topics), F32)],
        ),
        cost_estimate=pl.CostEstimate(flops=flops, bytes_accessed=20 * MIB, transcendentals=0),
        compiler_params=pltpu.CompilerParams(dimension_semantics=('arbitrary',), vmem_limit_bytes=56 * MIB),
        name='w_partial',
    )(idx, c, w, h_own, h_sib)


def h_kernel(tile, first, row_ref, c_ref, *refs):
    pieces, refs = refs[:8], refs[8:]
    ho_ref, hs_ref, refs = refs[0], refs[1], refs[2:]
    if not first:
        ik_ref, is_ref, refs = refs[0], refs[1], refs[2:]
    keep_ref, send_ref, w_ref = refs
    own = ho_ref.shape[0]

    @pl.when(pl.program_id(0) == 0)
    def _():
        for quarter in range(4):
            row = pl.multiple_of(row_ref[quarter] * 256, 256)
            w_ref[pl.ds(row, 128), :] = pieces[2 * quarter][...]
            w_ref[pl.ds(row + 128, 128), :] = pieces[2 * quarter + 1][...]

    h = jnp.concatenate([ho_ref[...], hs_ref[...]], axis=0)
    for t in range(c_ref.shape[0] // tile):
        rows = pl.ds(t * tile, tile)
        w = w_ref[rows, :]
        z = jnp.dot(w, h, preferred_element_type=F32)
        q = ratio(c_ref[rows, :], z)
        part = lax.dot_general(w, q, CONTRACT_DOCS, preferred_element_type=F32)
        if t == 0 and first:
            keep_ref[...] = part[:own]
            send_ref[...] = part[own:]
        elif t == 0:
            keep_ref[...] = ik_ref[...] + part[:own]
            send_ref[...] = is_ref[...] + part[own:]
        else:
            keep_ref[...] += part[:own]
            send_ref[...] += part[own:]


def h_partial(rows, c, pieces, h_own, h_sib, sums):
    docs, words = c.shape
    own, topics = h_own.shape[0], 2 * h_own.shape[0]
    width = 1024
    first = sums is None
    spec_h = pl.BlockSpec((own, width), lambda i, s: (0, i))
    in_specs = [pl.BlockSpec((docs, width), lambda i, s: (0, i))]
    in_specs += [pl.BlockSpec((128, topics), lambda i, s: (0, 0))] * 8
    in_specs += [spec_h] * (2 if first else 4)
    acc = jax.ShapeDtypeStruct((own, words), F32)
    return pl.pallas_call(
        functools.partial(h_kernel, 512, first),
        out_shape=(acc, acc, jax.ShapeDtypeStruct((docs, topics), BF16)),
        grid_spec=pltpu.PrefetchScalarGridSpec(
            num_scalar_prefetch=1,
            grid=(words // width,),
            in_specs=in_specs,
            out_specs=[spec_h, spec_h, pl.BlockSpec((docs, topics), lambda i, s: (0, 0))],
        ),
        input_output_aliases={} if first else {12: 0, 13: 1},
        cost_estimate=pl.CostEstimate(flops=4 * docs * words * topics, bytes_accessed=40 * MIB, transcendentals=0),
        compiler_params=pltpu.CompilerParams(dimension_semantics=('arbitrary',), vmem_limit_bytes=56 * MIB),
        name='h_partial',
    )(jnp.stack(rows), c, *pieces, h_own, h_sib, *(() if first else sums))


RS1A, RS1B, RS2A, RS2B, AY, AX, BX, BY, AF, BF = range(10)


def sweep_kernel(tile, c0, c1, c2, c3, wold_ref, ho_ref, hs_ref, wsh_ref, sh_ref,
                 keep_ref, send_ref, shard_ref, wout_ref, wsum_ref,
                 cbuf, wbuf, acc, sa, ka, sb, kb, ra, rb, r2a, r2b, wnew, csem, wsem, osem, ssem, rsem):
    c_refs = (c0, c1, c2, c3)
    j, x = lax.axis_index('y'), lax.axis_index('x')
    own = ho_ref.shape[0]
    words = ho_ref.shape[1]

    barrier = pltpu.get_barrier_semaphore()
    for axis, place in (('x', x), ('y', j)):
        pl.semaphore_signal(barrier, inc=1, device_id={axis: 1 - place}, device_id_type=MESH)
    pl.semaphore_wait(barrier, 2)

    def remote(src, dst, chunk, event, axis):
        other = 1 - (x if axis == 'x' else j)
        return pltpu.make_async_remote_copy(src_ref=src, dst_ref=dst, send_sem=ssem.at[chunk, event],
                                            recv_sem=rsem.at[chunk, event], device_id={axis: other},
                                            device_id_type=MESH)

    def rows_of(chunk, u, v, colour):
        return pl.ds(pl.multiple_of(chunk * 1024 + (2 * u + v) * 256 + colour * 128, 128), 128)

    def copy_of(event, chunk):
        if event == RS1A:
            return remote(sa.at[lax.rem(chunk, 2)], ra.at[chunk], chunk, event, 'x')
        if event == RS1B:
            return remote(sb.at[lax.rem(chunk, 2)], rb.at[chunk], chunk, event, 'y')
        if event == RS2A:
            return remote(ka.at[chunk, 0], r2a.at[chunk], chunk, event, 'y')
        if event == RS2B:
            return remote(kb.at[chunk, 0], r2b.at[chunk], chunk, event, 'x')
        if event in (AY, AX):
            part = wnew.at[rows_of(chunk, x, j, 0)]
            return remote(part, part, chunk, event, 'y' if event == AY else 'x')
        if event in (BX, BY):
            part = wnew.at[rows_of(chunk, x, j, 1)]
            return remote(part, part, chunk, event, 'y' if event == BY else 'x')
        if event == AF:
            part = wnew.at[rows_of(chunk, x, 1 - j, 0)]
            return remote(part, part, chunk, event, 'x')
        part = wnew.at[rows_of(chunk, 1 - x, j, 1)]
        return remote(part, part, chunk, event, 'y')

    def first_sums(chunk):
        copy_of(RS1A, chunk).wait_recv()
        ka[chunk] += ra[chunk]
        copy_of(RS2A, chunk).start()
        copy_of(RS1B, chunk).wait_recv()
        kb[chunk] += rb[chunk]
        copy_of(RS2B, chunk).start()

    def update(chunk):
        copy_of(RS2A, chunk).wait_recv()
        new = wsh_ref[chunk, 0] * (ka[chunk, 1] + r2a[chunk]) / sh_ref[...]
        shard_ref[chunk, 0] = new
        wnew[rows_of(chunk, x, j, 0), :] = new.astype(BF16)
        total = jnp.sum(new, axis=0, keepdims=True)
        copy_of(AY, chunk).start()
        copy_of(AX, chunk).start()
        copy_of(RS2B, chunk).wait_recv()
        new = wsh_ref[chunk, 1] * (kb[chunk, 1] + r2b[chunk]) / sh_ref[...]
        shard_ref[chunk, 1] = new
        wnew[rows_of(chunk, x, j, 1), :] = new.astype(BF16)
        wsum_ref[...] += total + jnp.sum(new, axis=0, keepdims=True)
        copy_of(BX, chunk).start()
        copy_of(BY, chunk).start()

    def forward(chunk):
        copy_of(AY, chunk).wait_recv()
        copy_of(AF, chunk).start()
        copy_of(BX, chunk).wait_recv()
        copy_of(BF, chunk).start()

    def arrived(chunk):
        for event in (AX, BY, AF, BF):
            copy_of(event, chunk).wait_recv()

    def quarter_of(step):
        u = jnp.where(step < 2, 1 - x, x)
        v = jnp.where(step % 2 == 0, 1 - j, j)
        return 2 * u + v

    def fetch_c(chunk, row, slot):
        for n in range(4):
            @pl.when(chunk == n)
            def _():
                pltpu.make_async_copy(c_refs[n].at[pl.ds(row, 256)], cbuf.at[slot], csem.at[slot]).start()

    def wait_c(slot):
        pltpu.make_async_copy(c_refs[0].at[pl.ds(0, 256)], cbuf.at[slot], csem.at[slot]).wait()

    def w_copy(chunk, row, slot):
        return pltpu.make_async_copy(wold_ref.at[pl.ds(chunk * 1024 + row, 256)], wbuf.at[slot], wsem.at[slot])

    def fetch_w_unit(unit, slot):
        chunk = unit // 4
        row = pl.multiple_of(quarter_of(lax.rem(unit, 4)) * 256, 256)
        fetch_c(chunk, row, slot)
        w_copy(chunk, row, slot).start()

    fetch_w_unit(jnp.int32(0), 0)
    for ref in (wsum_ref, keep_ref, send_ref):
        ref[...] = jnp.zeros_like(ref)

    def w_unit(unit, carry):
        chunk, step = unit // 4, lax.rem(unit, 4)
        slot = lax.rem(unit, 2)

        @pl.when(unit < 15)
        def _():
            fetch_w_unit(unit + 1, 1 - slot)

        @pl.when(unit == 15)
        def _():
            fetch_c(jnp.int32(0), 0, 1 - slot)

        wait_c(slot)
        w_copy(chunk, 0, slot).wait()
        for t in range(words // tile):
            cols = pl.ds(t * tile, tile)
            h = jnp.concatenate([ho_ref[:, cols], hs_ref[:, cols]], axis=0)
            z = jnp.dot(wbuf[slot], h, preferred_element_type=F32)
            q = ratio(cbuf[slot, :, cols], z)
            part = lax.dot_general(q, h, CONTRACT_WORDS, preferred_element_type=F32)
            if t == 0:
                acc[...] = part
            else:
                acc[...] += part

        @pl.when((chunk >= 2) & (step == 0))
        def _():
            copy_of(RS1A, chunk - 2).wait_send()
            copy_of(RS1B, chunk - 2).wait_send()

        pos = lax.rem(chunk, 2)

        @pl.when(step < 2)
        def _():
            sa[pos, step] = acc[:128]

        @pl.when(step >= 2)
        def _():
            ka[chunk, step - 2] = acc[:128]

        @pl.when(step % 2 == 0)
        def _():
            sb[pos, step // 2] = acc[128:]

        @pl.when(step % 2 == 1)
        def _():
            kb[chunk, step // 2] = acc[128:]

        @pl.when(step == 1)
        def _():
            copy_of(RS1A, chunk).start()

        @pl.when(step == 2)
        def _():
            copy_of(RS1B, chunk).start()

        @pl.when((step == 3) & (chunk >= 1))
        def _():
            first_sums(chunk - 1)
        return carry

    lax.fori_loop(0, 16, w_unit, 0)
    update(0)
    forward(0)
    first_sums(3)
    update(1)
    forward(1)
    update(2)

    def h_unit(unit, carry):
        chunk, step = unit // 4, lax.rem(unit, 4)
        slot = lax.rem(unit, 2)
        row = pl.multiple_of(step * 256, 256)

        @pl.when(unit < 15)
        def _():
            fetch_c((unit + 1) // 4, pl.multiple_of(lax.rem(unit + 1, 4) * 256, 256), 1 - slot)

        @pl.when(step == 0)
        def _():
            arrived(chunk)
            block = pl.ds(pl.multiple_of(chunk * 1024, 1024), 1024)
            pltpu.make_async_copy(wnew.at[block], wout_ref.at[block], osem.at[chunk]).start()

        wait_c(slot)
        w = wnew[pl.ds(pl.multiple_of(chunk * 1024 + row, 256), 256), :]
        for t in range(words // tile):
            cols = pl.ds(t * tile, tile)
            h = jnp.concatenate([ho_ref[:, cols], hs_ref[:, cols]], axis=0)
            z = jnp.dot(w, h, preferred_element_type=F32)
            q = ratio(cbuf[slot, :, cols], z)
            part = lax.dot_general(w, q, CONTRACT_DOCS, preferred_element_type=F32)

            keep_ref[:, cols] += part[:own]
            send_ref[:, cols] += part[own:]

        @pl.when(unit == 1)
        def _():
            update(3)

        @pl.when(unit == 3)
        def _():
            forward(2)

        @pl.when(unit == 5)
        def _():
            forward(3)
        return carry

    lax.fori_loop(0, 16, h_unit, 0)
    for chunk in range(4):
        block = pl.ds(chunk * 1024, 1024)
        pltpu.make_async_copy(wnew.at[block], wout_ref.at[block], osem.at[chunk]).wait()
        for event in range(10):
            if event > 1 or chunk > 1:
                copy_of(event, chunk).wait_send()


def fused_sweep(c_new, w_old, h_own, h_sib, shards, s_h):
    own, words = h_own.shape
    docs, topics = w_old.shape
    vmem, hbm = pl.BlockSpec(memory_space=pltpu.VMEM), pl.BlockSpec(memory_space=pl.ANY)
    acc = jax.ShapeDtypeStruct((own, words), F32)
    part = pltpu.VMEM((4, 2, 128, topics), F32)
    two = pltpu.VMEM((2, 2, 128, topics), F32)
    last = pltpu.VMEM((4, 128, topics), F32)
    dma = pltpu.SemaphoreType.DMA
    return pl.pallas_call(
        functools.partial(sweep_kernel, 1024),
        out_shape=(acc, acc, jax.ShapeDtypeStruct(shards.shape, F32), jax.ShapeDtypeStruct(w_old.shape, BF16),
                   jax.ShapeDtypeStruct((1, topics), F32)),
        in_specs=[hbm] * 5 + [vmem] * 4,
        out_specs=[vmem, vmem, vmem, hbm, vmem],
        scratch_shapes=[
            pltpu.VMEM((2, 256, words), BF16),
            pltpu.VMEM((2, 256, topics), BF16),
            pltpu.VMEM((256, topics), F32),
            two, part, two, part, part, part, last, last,
            pltpu.VMEM((docs, topics), BF16),
            dma((2,)), dma((2,)), dma((4,)), dma((4, 10)), dma((4, 10)),
        ],
        cost_estimate=pl.CostEstimate(flops=8 * docs * words * topics, bytes_accessed=100 * MIB, transcendentals=0),
        compiler_params=pltpu.CompilerParams(collective_id=0, has_side_effects=True, vmem_limit_bytes=67043328),
        name='fused_sweep',
    )(*c_new, w_old, h_own, h_sib, shards, s_h)


def swap(arr, axis):
    return lax.ppermute(arr, axis, [(0, 1), (1, 0)])


def flip(arr, k, axis):
    half = arr.shape[axis] // 2
    return jnp.where(k == 0, arr, jnp.roll(arr, half, axis=axis))


def first_sum(parts, other):
    keep_a, send_a, keep_b, send_b = parts
    got_a, got_b = swap(send_a, 'x'), swap(send_b, other)
    return (keep_a[0] + got_a[0], keep_b[0] + got_b[0]), (keep_a[1] + got_a[1], keep_b[1] + got_b[1])


def second_sum(mid, other):
    (next_a, next_b), (own_a, own_b) = mid
    return own_a + swap(next_a, other), own_b + swap(next_b, 'x')


def gather_pieces(own_a, own_b):
    a0, b0 = own_a.astype(BF16), own_b.astype(BF16)
    a1, b2 = swap(a0, 'y'), swap(b0, 'x')
    a2, b1 = swap(a0, 'x'), swap(b0, 'y')
    a3, b3 = swap(a1, 'x'), swap(b2, 'y')
    return [a0, b0, a1, b1, a2, b2, a3, b3]


def tie(value, *others):
    return lax.optimization_barrier((value,) + others)


def mesh_sum(vec):
    for axis in ('c', 'x', 'y'):
        vec = vec + swap(vec, axis)
    return vec


def local_sweeps(c_blk, w_loc, h_loc):
    j, x, k = (lax.axis_index(axis) for axis in ALL)
    diag = j == k
    docs, topics = w_loc.shape
    words = h_loc.shape[1]
    half = topics // 2
    chunk = docs // CHUNKS
    dev = lambda jj, xx, kk: jj * 4 + xx * 2 + kk
    trade_pairs = [(dev(a, b, 1 - a), dev(1 - a, b, a)) for a in range(2) for b in range(2)]

    def trade(arr):
        return jnp.where(diag, arr, lax.ppermute(arr, ALL, trade_pairs))

    def steps(u, v):
        return [2 * (1 - u) + 1 - v, 2 * (1 - u) + v, 2 * u + 1 - v, 2 * u + v]

    def w_phase(other, part_of, update):
        tag = jnp.zeros((), jnp.int32)
        parts, mids, shards = [], [], []
        for i in range(CHUNKS):
            if i >= 2:
                tag, parts[i - 2] = tie(tag, parts[i - 2])
                mids.append(first_sum(parts[i - 2], other))
                if i >= 3:
                    shards.append(update(i - 3, second_sum(mids[i - 3], other)))
                    tag, mids[-1], shards[-1] = tie(tag, mids[-1], shards[-1])
                else:
                    tag, mids[-1] = tie(tag, mids[-1])
            parts.append(part_of(i, tag))
        return tag, parts, mids, shards

    def finish(other, i, parts, mids, shards, update):
        if len(mids) < CHUNKS:
            mids.append(first_sum(parts[len(mids)], other))
        if len(shards) < len(mids) and len(shards) < CHUNKS:
            n = len(shards)
            shards.append(update(n, second_sum(mids[n], other)))

    early = [trade(c_blk[i * chunk:(i + 1) * chunk]) for i in range(2)]
    h_bf = h_loc.astype(BF16)
    w_bf = w_loc.astype(BF16)
    s_h = jnp.sum(h_loc, axis=1)
    s_h = s_h + swap(s_h, 'c')
    s_h = s_h + swap(s_h, 'x')

    def part_of(i, tag):
        return w_partial(steps(x, k), c_blk, w_bf, h_bf[:half], h_bf[half:], (4 * i + tag, 4 * i + tag))

    def update(i, sums):
        row = i * chunk + 256 * (2 * x + k)
        w_a = lax.dynamic_slice_in_dim(w_loc, row, 128, 0) * sums[0] / s_h
        w_b = lax.dynamic_slice_in_dim(w_loc, row + 128, 128, 0) * sums[1] / s_h
        both = flip(trade(jnp.stack([w_a, w_b])), k, 2)
        return both[0], both[1]

    tag, parts, mids, shards = w_phase('c', part_of, update)
    while len(shards) < CHUNKS:
        finish('c', 0, parts, mids, shards, update)
    h_rel = flip(jnp.where(diag, h_loc, swap(h_loc, 'c')), k, 0)
    h_own = h_rel[:half]
    h_bf_own, h_bf_sib = h_own.astype(BF16), h_rel[half:].astype(BF16)
    pieces = [gather_pieces(*shard) for shard in shards]
    c_late, pieces[-1][6] = tie(c_blk, pieces[-1][6])
    c_new = early + [trade(c_late[i * chunk:(i + 1) * chunk]) for i in range(2, CHUNKS)]

    for sweep in range(SWEEPS):
        if sweep == 0:
            rows = steps(x, j)[::-1]
            sums, w_full = None, []
            for i in range(CHUNKS):
                keep, send, w_chunk = h_partial(rows, c_new[i], pieces[i], h_bf_own, h_bf_sib, sums)
                sums = keep, send
                w_full.append(w_chunk)
            w_full = jnp.concatenate(w_full)
            w_sum = sum(jnp.sum(w_a + w_b, axis=0) for w_a, w_b in shards)
            shards = jnp.stack([jnp.stack(shard) for shard in shards])
        else:
            h_sum = jnp.sum(h_own, axis=1)
            h_sum = flip(jnp.concatenate([h_sum, jnp.zeros_like(h_sum)]), k, 0)
            s_h = flip(mesh_sum(h_sum), k, 0)
            keep, send, shards, w_full, w_sum = fused_sweep(c_new, w_full, h_bf_own, h_bf_sib, shards, s_h[None])
            w_sum = w_sum[0]
        s_w = flip(mesh_sum(flip(w_sum, k, 0)), k, 0)[:half]
        h_own = h_own * (keep + swap(send, 'c')) / s_w[:, None]
        if sweep < SWEEPS - 1:
            h_bf_own = h_own.astype(BF16)
            h_bf_sib = swap(h_bf_own, 'c')

    own = flip(shards, k, 3)
    into = [(dev(1 - a, b, a), dev(a, b, a)) for a in range(2) for b in range(2)]
    cross = [(dev(a, b, a), dev(a, 1 - b, a)) for a in range(2) for b in range(2)]
    aside = [(dev(a, b, a), dev(a, b, 1 - a)) for a in range(2) for b in range(2)]
    from_y = lax.ppermute(own, ALL, into)
    from_x = lax.ppermute(own, ALL, cross)
    from_xy = lax.ppermute(from_y, ALL, cross)
    near = jnp.where(j == 0, jnp.stack([own, from_y], 1), jnp.stack([from_y, own], 1))
    far = jnp.where(j == 0, jnp.stack([from_x, from_xy], 1), jnp.stack([from_xy, from_x], 1))
    w_half = jnp.where(x == 0, jnp.stack([near, far], 1), jnp.stack([far, near], 1)).reshape(docs, topics)
    w_out = jnp.where(diag, w_half, lax.ppermute(w_half, ALL, aside))

    from_y = swap(h_own, 'y')
    mine = jnp.where(diag, h_own, from_y)
    other = swap(jnp.where(diag, from_y, h_own), 'c')
    h_out = jnp.where(k == 0, jnp.concatenate([mine, other]), jnp.concatenate([other, mine]))
    return w_out, h_out


def solution(mesh):
    fine = Mesh(mesh.devices.reshape(2, 2, 2), ALL)
    spec_c = P('y', ('x', 'c'))
    spec_w = P('y', None)
    spec_h = P(None, ('x', 'c'))
    return jax.shard_map(local_sweeps, mesh=fine, in_specs=(spec_c, spec_w, spec_h), out_specs=(spec_w, spec_h), check_vma=False)
```

time: 2720 us -> 1800 us (0.66)
  waiting for transfers between devices: 1940 us -> 607 us
  Pallas kernels: 0 us -> 767 us
  matrix products: 593 us -> 0 us
  starting transfers between devices: 0.33 us -> 157 us
  local copies, waits for them, and re-layouts: 1.83 us -> 75.2 us
  other arithmetic: 120 us -> 186 us
  blocking collectives: 41.3 us -> 0 us
    psum x8 -> x0, waiting for transfers between devices: 1940 us -> none  [the longest x4 1120 us: local_sweeps(): lax.psum(lax.dot_general(w_bf, q_blk, CONTRACT_DOCS, preferred_element_ty...]
    pallas_call x0 -> x11, Pallas kernels: none -> 767 us  [the longest x3 600 us: fused_sweep(): pl.pallas_call(functools.partial(sweep_kernel, 1024), out_shape=(acc, acc...]
    ppermute x0 -> x85, waiting for transfers between devices: none -> 607 us  [the longest x8 294 us: trade(): return jnp.where(diag, arr, lax.ppermute(arr, ALL, trade_pairs))]
    dot_general x16 -> x0, matrix products: 593 us -> none  [the longest x8 309 us: ratio_block(): z_blk = jnp.dot(w_bf, h_bf, preferred_element_type=jnp.float32)]
    ppermute x0 -> x85, starting transfers between devices: none -> 157 us  [the longest x73 119 us: swap(): return lax.ppermute(arr, axis, [(0, 1), (1, 0)])]
    select_n x0 -> x35, other arithmetic: none -> 114 us  [the longest x8 48.4 us: trade(): return jnp.where(diag, arr, lax.ppermute(arr, ALL, trade_pairs))]
    reduce_sum x8 -> x6, other arithmetic: 105 us -> 22.1 us  [the longest x3 20.4 us: local_sweeps(): h_sum = jnp.sum(h_own, axis=1)]
    psum x8 -> x0, blocking collectives: 41.3 us -> none  [the longest x4 25.4 us: local_sweeps(): s_h = lax.psum(jnp.sum(h_loc, axis=1), 'col')]
  transfers between devices with their start and end apart: 8 -> 85, of which waited for: 8 -> 39; matrix products, arithmetic and copies ran while one was open for 0% -> 10% of each run, Pallas kernels for 0% -> 5%
where the time goes in v1:
time: 1800 us; the launch traced here: 1790 us
  Pallas kernels  767 us (43%)
  waiting for transfers between devices  607 us (34%)
  other arithmetic  186 us (10%)
  starting transfers between devices  157 us (9%)
  local copies, waits for them, and re-layouts  75.2 us (4%)
    pallas_call x3, Pallas kernels, fused_sweep(): pl.pallas_call(functools.partial(sweep_kernel, 1024), out_shape=(acc, acc...  600 us
    ppermute x8, waiting for transfers between devices, trade(): return jnp.where(diag, arr, lax.ppermute(arr, ALL, trade_pairs))  294 us
    ppermute x73, waiting for transfers between devices, swap(): return lax.ppermute(arr, axis, [(0, 1), (1, 0)])  285 us
    ppermute x73, starting transfers between devices, swap(): return lax.ppermute(arr, axis, [(0, 1), (1, 0)])  119 us
    pallas_call x4, Pallas kernels, w_partial(): pl.pallas_call(functools.partial(w_kernel, 1024), out_shape=(part,) * 4,...  83.8 us
    pallas_call x4, Pallas kernels, h_partial(): pl.pallas_call(functools.partial(h_kernel, 512, first), out_shape=(acc, a...  83.5 us
    select_n x8, other arithmetic, trade(): return jnp.where(diag, arr, lax.ppermute(arr, ALL, trade_pairs))  48.4 us
  transfers between devices with their start and end apart: 85, of which 39 were waited for; matrix products, arithmetic and copies ran while one was open for 10% of the time, Pallas kernels for 5%

profile of v1, /device:TPU:1, one launch (start us, length us, event | category | flops | bytes accessed | tf_op | source)
XLA Modules:
  0.0 1794.4 jit_solution(17710563872836091636)
XLA Ops:
  0.7 7.9 convert_element_type.55.w_ref
  9.2 10.5 collective-permute-done.26
  19.8 17.2 broadcast_select_fusion.4
  40.1 20.9 %w_partial.4 = (f32[2,128,768]{2,1,0:T(8,128)}, f32[2,128,768]{2,1,0:T(8,128)}, f32[2,128,768]{2,1,0:T(8,128)}, f32[2,128,768]{2,1,0:T(8,128)}) custom-call(s32[8]{0:T(128)} %stack.211.idx_ref, bf16[4096,4096]{1,0:T(8,128)(2,1)} %c_ref.7, bf16[4096,768]{1,0:T(8,128)(2,1)} %convert_element_type.55.w_ref, bf16[384,4096]{1,0:T(8,128)(2,1)} %get-tuple-element.168.ho_ref, ...), custom_call_target="tpu_custom_call" | custom-call | flops 12884901888 | bytes 20971520 | tf_op jit(solution)/shard_map/w_partial/pallas_call | solution.py:65
  64.0 17.0 collective-permute-done.2
  85.5 20.9 %w_partial.7 = (f32[2,128,768]{2,1,0:T(8,128)}, f32[2,128,768]{2,1,0:T(8,128)}, f32[2,128,768]{2,1,0:T(8,128)}, f32[2,128,768]{2,1,0:T(8,128)}) custom-call(s32[8]{0:T(128)} %stack.240.idx_ref, bf16[4096,4096]{1,0:T(8,128)(2,1)} %c_ref.7, bf16[4096,768]{1,0:T(8,128)(2,1)} %convert_element_type.55.w_ref, bf16[384,4096]{1,0:T(8,128)(2,1)} %get-tuple-element.168.ho_ref, ...), custom_call_target="tpu_custom_call" | custom-call | flops 12884901888 | bytes 20971520 | tf_op jit(solution)/shard_map/w_partial/pallas_call | solution.py:65
  113.1 11.5 collective-permute-done.36
  134.0 21.1 %w_partial.5 = (f32[2,128,768]{2,1,0:T(8,128)}, f32[2,128,768]{2,1,0:T(8,128)}, f32[2,128,768]{2,1,0:T(8,128)}, f32[2,128,768]{2,1,0:T(8,128)}) custom-call(s32[8]{0:T(128)} %stack.216.idx_ref, bf16[4096,4096]{1,0:T(8,128)(2,1)} %c_ref.7, bf16[4096,768]{1,0:T(8,128)(2,1)} %convert_element_type.55.w_ref, bf16[384,4096]{1,0:T(8,128)(2,1)} %get-tuple-element.168.ho_ref, ...), custom_call_target="tpu_custom_call" | custom-call | flops 12884901888 | bytes 20971520 | tf_op jit(solution)/shard_map/w_partial/pallas_call | solution.py:65
  160.4 3.3 collective-permute-start.10
  163.7 10.3 collective-permute-done.4
  180.5 20.9 %w_partial.6 = (f32[2,128,768]{2,1,0:T(8,128)}, f32[2,128,768]{2,1,0:T(8,128)}, f32[2,128,768]{2,1,0:T(8,128)}, f32[2,128,768]{2,1,0:T(8,128)}) custom-call(s32[8]{0:T(128)} %stack.224.idx_ref, bf16[4096,4096]{1,0:T(8,128)(2,1)} %c_ref.7, bf16[4096,768]{1,0:T(8,128)(2,1)} %convert_element_type.55.w_ref, bf16[384,4096]{1,0:T(8,128)(2,1)} %get-tuple-element.168.ho_ref, ...), custom_call_target="tpu_custom_call" | custom-call | flops 12884901888 | bytes 20971520 | tf_op jit(solution)/shard_map/w_partial/pallas_call | solution.py:65
  202.9 7.9 slice.301
  221.2 3.4 collective-permute-start.12
  228.0 9.5 collective-permute-done.14
  240.8 3.7 collective-permute-start.15
  244.5 69.4 %collective-permute-done.15 = f32[2,128,768]{2,1,0:T(8,128)S(1)} collective-permute-done((f32[2,128,768]{2,1,0:T(8,128)S(1)}, f32[2,128,768]{2,1,0:T(8,128)S(1)}, u32[]{:S(2)}, u32[]{:S(2)}) %collective-permute-start.15) | collective-permute-done | bytes 786464 | tf_op jit(solution)/shard_map/ppermute | solution.py:453
  316.6 6.7 collective-permute-done.16.refs_2_
  325.4 4.5 collective-permute-done.17.refs_6_
  329.9 7.9 slice.336
  340.9 14.3 broadcast_select_fusion.2
  355.2 3.3 collective-permute-start
  358.6 10.7 fusion.45
  369.2 63.3 %collective-permute-done.19 = bf16[1024,4096]{1,0:T(8,128)(2,1)} collective-permute-done((bf16[1024,4096]{1,0:T(8,128)(2,1)}, bf16[1024,4096]{1,0:T(8,128)(2,1)}, u32[]{:S(2)}, u32[]{:S(2)}) %collective-permute-start.19) | collective-permute-done | bytes 8388640 | tf_op jit(solution)/shard_map/ppermute | solution.py:453
  432.5 14.5 broadcast_select_fusion
  454.7 6.8 collective-permute-start.40
  461.5 3.6 fusion.44
  469.4 153.4 %collective-permute-done.40 = f32[2,128,768]{2,1,0:T(8,128)} collective-permute-done((f32[2,128,768]{2,1,0:T(8,128)}, f32[2,128,768]{2,1,0:T(8,128)}, u32[]{:S(2)}, u32[]{:S(2)}) %collective-permute-start.40) | collective-permute-done | bytes 786464 | tf_op jit(solution)/shard_map/ppermute | solution.py:453
  628.0 8.1 collective-permute-done.29
  641.1 3.6 collective-permute-done.20.refs_2_
  649.0 9.0 broadcast_select_fusion.3.c_ref.c0
  661.1 19.3 %h_partial.4 = (f32[384,4096]{1,0:T(8,128)}, f32[384,4096]{1,0:T(8,128)}, bf16[1024,768]{1,0:T(8,128)(2,1)}) custom-call(s32[4]{0:T(128)} %pad_add_fusion.row_ref, bf16[1024,4096]{1,0:T(8,128)(2,1)} %broadcast_select_fusion.3.c_ref.c0, bf16[128,768]{1,0:T(8,128)(2,1)} %copy-done.32, bf16[128,768]{1,0:T(8,128)(2,1)} %copy-done.31, ...), custom_call_target="tpu_custom_call" | custom-call | flops 12884901888 | bytes 41943040 | tf_op jit(solution)/shard_map/h_partial/pallas_call | solution.py:134
  684.0 21.3 %h_partial.5 = (f32[384,4096]{1,0:T(8,128)}, f32[384,4096]{1,0:T(8,128)}, bf16[1024,768]{1,0:T(8,128)(2,1)}) custom-call(s32[4]{0:T(128)} %pad_add_fusion.row_ref, bf16[1024,4096]{1,0:T(8,128)(2,1)} %get-tuple-element.148.c_ref.c1, bf16[128,768]{1,0:T(8,128)(2,1)} %copy-done.39, ...), custom_call_target="tpu_custom_call", output_to_operand_aliasing={{0}: (12, {}), {1}: (13, {})} | custom-call | flops 12884901888 | bytes 41943040 | tf_op jit(solution)/shard_map/h_partial/pallas_call | solution.py:134
  706.2 9.0 broadcast_select_fusion.1.c_ref.c2
  718.2 21.2 %h_partial.6 = (f32[384,4096]{1,0:T(8,128)}, f32[384,4096]{1,0:T(8,128)}, bf16[1024,768]{1,0:T(8,128)(2,1)}) custom-call(s32[4]{0:T(128)} %pad_add_fusion.row_ref, bf16[1024,4096]{1,0:T(8,128)(2,1)} %broadcast_select_fusion.1.c_ref.c2, bf16[128,768]{1,0:T(8,128)(2,1)} %copy-done.37, ...), custom_call_target="tpu_custom_call", output_to_operand_aliasing={{0}: (12, {}), {1}: (13, {})} | custom-call | flops 12884901888 | bytes 41943040 | tf_op jit(solution)/shard_map/h_partial/pallas_call | solution.py:134
  740.2 21.7 %h_partial.7 = (f32[384,4096]{1,0:T(8,128)}, f32[384,4096]{1,0:T(8,128)}, bf16[1024,768]{1,0:T(8,128)(2,1)}) custom-call(s32[4]{0:T(128)} %pad_add_fusion.row_ref, bf16[1024,4096]{1,0:T(8,128)(2,1)} %get-tuple-element.146.c_ref.c3, bf16[128,768]{1,0:T(8,128)(2,1)} %copy-done.34, ...), custom_call_target="tpu_custom_call", output_to_operand_aliasing={{0}: (12, {}), {1}: (13, {})} | custom-call | flops 12884901888 | bytes 41943040 | tf_op jit(solution)/shard_map/h_partial/pallas_call | solution.py:134
  761.9 5.2 collective-permute-start.51
  767.4 9.6 collective-permute-done.52
  782.1 5.5 fusion.43
  790.7 5.2 collective-permute-done.56
  803.6 200.2 %fused_sweep.3 = (f32[384,4096]{1,0:T(8,128)}, f32[384,4096]{1,0:T(8,128)}, f32[4,2,128,768]{3,2,1,0:T(8,128)}, bf16[4096,768]{1,0:T(8,128)(2,1)}, f32[1,768]{1,0:T(1,128)}) custom-call(bf16[1024,4096]{1,0:T(8,128)(2,1)} %broadcast_select_fusion.3.c_ref.c0, bf16[1024,4096]{1,0:T(8,128)(2,1)} %get-tuple-element.148.c_ref.c1, ...), custom_call_target="tpu_custom_call" | custom-call | flops 103079215104 | bytes 104857600 | tf_op jit(solution)/shard_map/fused_sweep/pallas_call | solution.py:384
  1003.9 4.7 collective-permute-start.59
  1010.0 8.3 collective-permute-done.60
  1023.3 7.4 fusion.42
  1038.3 5.3 collective-permute-done.64
  1050.8 199.9 %fused_sweep.4 = (f32[384,4096]{1,0:T(8,128)}, f32[384,4096]{1,0:T(8,128)}, f32[4,2,128,768]{3,2,1,0:T(8,128)}, bf16[4096,768]{1,0:T(8,128)(2,1)}, f32[1,768]{1,0:T(1,128)}) custom-call(bf16[1024,4096]{1,0:T(8,128)(2,1)} %broadcast_select_fusion.3.c_ref.c0, bf16[1024,4096]{1,0:T(8,128)(2,1)} %get-tuple-element.148.c_ref.c1, ...), custom_call_target="tpu_custom_call" | custom-call | flops 103079215104 | bytes 104857600 | tf_op jit(solution)/shard_map/fused_sweep/pallas_call | solution.py:384
  1250.7 4.8 collective-permute-start.67
  1256.9 8.3 collective-permute-done.68
  1270.2 7.4 fusion.41
  1285.1 5.3 collective-permute-done.72
  1297.6 199.9 %fused_sweep.5 = (f32[384,4096]{1,0:T(8,128)}, f32[384,4096]{1,0:T(8,128)}, f32[4,2,128,768]{3,2,1,0:T(8,128)}, bf16[4096,768]{1,0:T(8,128)(2,1)}, f32[1,768]{1,0:T(1,128)}) custom-call(bf16[1024,4096]{1,0:T(8,128)(2,1)} %broadcast_select_fusion.3.c_ref.c0, bf16[1024,4096]{1,0:T(8,128)(2,1)} %get-tuple-element.148.c_ref.c1, ...), custom_call_target="tpu_custom_call" | custom-call | flops 103079215104 | bytes 104857600 | tf_op jit(solution)/shard_map/fused_sweep/pallas_call | solution.py:384
  1500.7 4.1 collective-permute-start.75
  1509.1 28.1 %collective-permute-done.75 = f32[4,2,128,768]{3,2,1,0:T(8,128)} collective-permute-done((f32[4,2,128,768]{3,2,1,0:T(8,128)S(1)}, f32[4,2,128,768]{3,2,1,0:T(8,128)}, u32[]{:S(2)}, u32[]{:S(2)}) %collective-permute-start.75) | collective-permute-done | bytes 3145760 | tf_op jit(solution)/shard_map/ppermute | solution.py:534
  1539.7 7.7 collective-permute-start.80
  1551.1 31.6 %collective-permute-start.82 = (f32[768]{0:T(1024)S(1)}, f32[768]{0:T(1024)S(1)}, u32[]{:S(2)}, u32[]{:S(2)}) collective-permute-start(f32[768]{0:T(1024)S(1)} %add.489), channel_id=1, source_target_pairs={{0,4},{4,0},{1,5},{5,1},{2,6},{6,2},{3,7},{7,3}} | collective-permute-start | bytes 9224 | tf_op jit(solution)/shard_map/ppermute | solution.py:405
  1583.7 3.4 maximum_select_fusion.3
  1587.1 5.9 maximum_select_fusion.4
  1593.1 5.3 maximum_select_fusion.1
  1598.4 10.7 copy.11
  1610.5 9.5 multiply_divide_fusion
  1620.0 8.8 collective-permute-start.83
  1628.8 135.2 %collective-permute-done.83 = f32[384,4096]{1,0:T(8,128)} collective-permute-done((f32[384,4096]{1,0:T(8,128)}, f32[384,4096]{1,0:T(8,128)}, u32[]{:S(2)}, u32[]{:S(2)}) %collective-permute-start.83) | collective-permute-done | bytes 6291488 | tf_op jit(solution)/shard_map/ppermute | solution.py:405
  1763.9 8.9 broadcast_select_fusion.7
  1774.2 14.0 broadcast_select_fusion.5
  1788.2 5.7 maximum_select_fusion.2
  (385 shorter events, 178.4 us)
Async XLA Ops:
  0.6 19.1 %collective-permute-start.26 = (f32[768,4096]{1,0:T(8,128)}, f32[768,4096]{1,0:T(8,128)}, u32[]{:S(2)}, u32[]{:S(2)}) collective-permute-start(f32[768,4096]{1,0:T(8,128)} %param.5), channel_id=1, source_target_pairs={{0,1},{1,0},{2,3},{3,2},{4,5},{5,4},{6,7},{7,6}} | collective-permute-start | bytes 37748744 | tf_op jit(solution)/shard_map/ppermute | solution.py:405
  61.0 20.0 %collective-permute-start.2 = (f32[2,128,768]{2,1,0:T(8,128)}, f32[2,128,768]{2,1,0:T(8,128)S(1)}, u32[]{:S(2)}, u32[]{:S(2)}) collective-permute-start(f32[2,128,768]{2,1,0:T(8,128)} %get-tuple-element.74), channel_id=1, source_target_pairs={{0,2},{2,0},{1,3},{3,1},{4,6},{6,4},{5,7},{7,5}} | collective-permute-start | bytes 2359304 | tf_op jit(solution)/shard_map/ppermute | solution.py:405
  63.4 19.6 %collective-permute-start.3 = (f32[2,128,768]{2,1,0:T(8,128)}, f32[2,128,768]{2,1,0:T(8,128)S(1)}, u32[]{:S(2)}, u32[]{:S(2)}) collective-permute-start(f32[2,128,768]{2,1,0:T(8,128)} %get-tuple-element.76), channel_id=1, source_target_pairs={{0,1},{1,0},{2,3},{3,2},{4,5},{5,4},{6,7},{7,6}} | collective-permute-start | bytes 2359304 | tf_op jit(solution)/shard_map/ppermute | solution.py:405
  106.4 18.2 %collective-permute-start.36 = (f32[2,128,768]{2,1,0:T(8,128)}, f32[2,128,768]{2,1,0:T(8,128)S(1)}, u32[]{:S(2)}, u32[]{:S(2)}) collective-permute-start(f32[2,128,768]{2,1,0:T(8,128)} %get-tuple-element.108), channel_id=1, source_target_pairs={{0,2},{2,0},{1,3},{3,1},{4,6},{6,4},{5,7},{7,5}} | collective-permute-start | bytes 2359304 | tf_op jit(solution)/shard_map/ppermute | solution.py:405
  107.6 22.2 %collective-permute-start.38 = (f32[2,128,768]{2,1,0:T(8,128)}, f32[2,128,768]{2,1,0:T(8,128)S(1)}, u32[]{:S(2)}, u32[]{:S(2)}) collective-permute-start(f32[2,128,768]{2,1,0:T(8,128)} %get-tuple-element.110), channel_id=1, source_target_pairs={{0,1},{1,0},{2,3},{3,2},{4,5},{5,4},{6,7},{7,6}} | collective-permute-start | bytes 2359304 | tf_op jit(solution)/shard_map/ppermute | solution.py:405
  111.0 44.1 %collective-permute-start.8 = (f32[768]{0:T(1024)S(1)}, f32[768]{0:T(1024)S(1)}, u32[]{:S(2)}, u32[]{:S(2)}) collective-permute-start(f32[768]{0:T(1024)S(1)} %add.412), channel_id=1, source_target_pairs={{0,2},{2,0},{1,3},{3,1},{4,6},{6,4},{5,7},{7,5}} | collective-permute-start | bytes 9224 | tf_op jit(solution)/shard_map/ppermute | solution.py:405
  111.0 44.2 %collective-permute-start.6 = (f32[128,768]{1,0:T(8,128)}, f32[128,768]{1,0:T(8,128)S(1)}, u32[]{:S(2)}, u32[]{:S(2)}) collective-permute-start(f32[128,768]{1,0:T(8,128)} %get-tuple-element.88), channel_id=1, source_target_pairs={{0,1},{1,0},{2,3},{3,2},{4,5},{5,4},{6,7},{7,6}} | collective-permute-start | bytes 1179656 | tf_op jit(solution)/shard_map/ppermute | solution.py:405
  111.7 44.0 %collective-permute-start.9 = (f32[128,768]{1,0:T(8,128)}, f32[128,768]{1,0:T(8,128)S(1)}, u32[]{:S(2)}, u32[]{:S(2)}) collective-permute-start(f32[128,768]{1,0:T(8,128)} %get-tuple-element.90), channel_id=1, source_target_pairs={{0,2},{2,0},{1,3},{3,1},{4,6},{6,4},{5,7},{7,5}} | collective-permute-start | bytes 1179656 | tf_op jit(solution)/shard_map/ppermute | solution.py:405
  126.7 29.0 %collective-permute-start.37 = (f32[128,768]{1,0:T(8,128)}, f32[128,768]{1,0:T(8,128)S(1)}, u32[]{:S(2)}, u32[]{:S(2)}) collective-permute-start(f32[128,768]{1,0:T(8,128)} %fusion.6), channel_id=1, source_target_pairs={{0,1},{1,0},{2,3},{3,2},{4,5},{5,4},{6,7},{7,6}} | collective-permute-start | bytes 1179656 | tf_op jit(solution)/shard_map/ppermute | solution.py:405
  132.5 24.7 %collective-permute-start.39 = (f32[128,768]{1,0:T(8,128)}, f32[128,768]{1,0:T(8,128)}, u32[]{:S(2)}, u32[]{:S(2)}) collective-permute-start(f32[128,768]{1,0:T(8,128)} %fusion), channel_id=1, source_target_pairs={{0,2},{2,0},{1,3},{3,1},{4,6},{6,4},{5,7},{7,5}} | collective-permute-start | bytes 1179656 | tf_op jit(solution)/shard_map/ppermute | solution.py:405
  155.1 18.9 %collective-permute-start.4 = (f32[2,128,768]{2,1,0:T(8,128)}, f32[2,128,768]{2,1,0:T(8,128)}, u32[]{:S(2)}, u32[]{:S(2)}) collective-permute-start(f32[2,128,768]{2,1,0:T(8,128)} %get-tuple-element.84), channel_id=1, source_target_pairs={{0,2},{2,0},{1,3},{3,1},{4,6},{6,4},{5,7},{7,5}} | collective-permute-start | bytes 2359304 | tf_op jit(solution)/shard_map/ppermute | solution.py:405
  155.2 21.0 %collective-permute-start.5 = (f32[2,128,768]{2,1,0:T(8,128)}, f32[2,128,768]{2,1,0:T(8,128)}, u32[]{:S(2)}, u32[]{:S(2)}) collective-permute-start(f32[2,128,768]{2,1,0:T(8,128)} %get-tuple-element.86), channel_id=1, source_target_pairs={{0,1},{1,0},{2,3},{3,2},{4,5},{5,4},{6,7},{7,6}} | collective-permute-start | bytes 2359304 | tf_op jit(solution)/shard_map/ppermute | solution.py:405
  160.4 18.2 %collective-permute-start.10 = (f32[2,128,768]{2,1,0:T(8,128)S(1)}, f32[2,128,768]{2,1,0:T(8,128)S(1)}, u32[]{:S(2)}, u32[]{:S(2)}) collective-permute-start(f32[2,128,768]{2,1,0:T(8,128)S(1)} %pad_maximum_fusion.2), channel_id=1, source_target_pairs={{1,4},{3,6},{4,1},{6,3}} | collective-permute-start | bytes 2359304 | tf_op jit(solution)/shard_map/ppermute | solution.py:453
  201.4 18.1 %collective-permute-start.11 = (f32[2,128,768]{2,1,0:T(8,128)}, f32[2,128,768]{2,1,0:T(8,128)S(1)}, u32[]{:S(2)}, u32[]{:S(2)}) collective-permute-start(f32[2,128,768]{2,1,0:T(8,128)} %get-tuple-element.93), channel_id=1, source_target_pairs={{0,2},{2,0},{1,3},{3,1},{4,6},{6,4},{5,7},{7,5}} | collective-permute-start | bytes 2359304 | tf_op jit(solution)/shard_map/ppermute | solution.py:405
  201.7 22.9 %collective-permute-start.13 = (f32[2,128,768]{2,1,0:T(8,128)}, f32[2,128,768]{2,1,0:T(8,128)S(1)}, u32[]{:S(2)}, u32[]{:S(2)}) collective-permute-start(f32[2,128,768]{2,1,0:T(8,128)} %get-tuple-element.95), channel_id=1, source_target_pairs={{0,1},{1,0},{2,3},{3,2},{4,5},{5,4},{6,7},{7,6}} | collective-permute-start | bytes 2359304 | tf_op jit(solution)/shard_map/ppermute | solution.py:405
  210.8 130.1 %collective-permute-start.1 = (bf16[1024,4096]{1,0:T(8,128)(2,1)}, bf16[1024,4096]{1,0:T(8,128)(2,1)}, u32[]{:S(2)}, u32[]{:S(2)}) collective-permute-start(bf16[1024,4096]{1,0:T(8,128)(2,1)} %slice.301), channel_id=1, source_target_pairs={{1,4},{3,6},{4,1},{6,3}} | collective-permute-start | bytes 25165832 | tf_op jit(solution)/shard_map/ppermute | solution.py:453
  214.1 12.4 collective-permute-start.27
  214.9 13.1 collective-permute-start.28
  221.2 6.8 collective-permute-start.12
  226.3 11.2 collective-permute-start.14
  240.8 73.1 %collective-permute-start.15 = (f32[2,128,768]{2,1,0:T(8,128)S(1)}, f32[2,128,768]{2,1,0:T(8,128)S(1)}, u32[]{:S(2)}, u32[]{:S(2)}) collective-permute-start(f32[2,128,768]{2,1,0:T(8,128)S(1)} %pad_maximum_fusion.3), channel_id=1, source_target_pairs={{1,4},{3,6},{4,1},{6,3}} | collective-permute-start | bytes 2359304 | tf_op jit(solution)/shard_map/ppermute | solution.py:453
  316.6 6.7 collective-permute-start.16
  337.8 94.8 %collective-permute-start.19 = (bf16[1024,4096]{1,0:T(8,128)(2,1)}, bf16[1024,4096]{1,0:T(8,128)(2,1)}, u32[]{:S(2)}, u32[]{:S(2)}) collective-permute-start(bf16[1024,4096]{1,0:T(8,128)(2,1)} %slice.336), channel_id=1, source_target_pairs={{1,4},{3,6},{4,1},{6,3}} | collective-permute-start | bytes 25165832 | tf_op jit(solution)/shard_map/ppermute | solution.py:453
  355.2 293.8 %collective-permute-start = (bf16[1024,4096]{1,0:T(8,128)(2,1)}, bf16[1024,4096]{1,0:T(8,128)(2,1)}, u32[]{:S(2)}, u32[]{:S(2)}) collective-permute-start(bf16[1024,4096]{1,0:T(8,128)(2,1)} %get-tuple-element.149), channel_id=1, source_target_pairs={{1,4},{3,6},{4,1},{6,3}} | collective-permute-start | bytes 25165832 | tf_op jit(solution)/shard_map/ppermute | solution.py:453
  447.0 258.3 %collective-permute-start.18 = (bf16[1024,4096]{1,0:T(8,128)(2,1)}, bf16[1024,4096]{1,0:T(8,128)(2,1)}, u32[]{:S(2)}, u32[]{:S(2)}) collective-permute-start(bf16[1024,4096]{1,0:T(8,128)(2,1)} %get-tuple-element.147), channel_id=1, source_target_pairs={{1,4},{3,6},{4,1},{6,3}} | collective-permute-start | bytes 25165832 | tf_op jit(solution)/shard_map/ppermute | solution.py:453
  454.7 168.2 %collective-permute-start.40 = (f32[2,128,768]{2,1,0:T(8,128)}, f32[2,128,768]{2,1,0:T(8,128)}, u32[]{:S(2)}, u32[]{:S(2)}) collective-permute-start(f32[2,128,768]{2,1,0:T(8,128)} %pad_maximum_fusion.5), channel_id=1, source_target_pairs={{1,4},{3,6},{4,1},{6,3}} | collective-permute-start | bytes 2359304 | tf_op jit(solution)/shard_map/ppermute | solution.py:453
  466.7 171.4 %collective-permute-start.23 = (bf16[128,768]{1,0:T(8,128)(2,1)S(1)}, bf16[128,768]{1,0:T(8,128)(2,1)S(1)}, u32[]{:S(2)}, u32[]{:S(2)}) collective-permute-start(bf16[128,768]{1,0:T(8,128)(2,1)S(1)} %get-tuple-element.196.refs_1_), channel_id=1, source_target_pairs={{0,2},{2,0},{1,3},{3,1},{4,6},{6,4},{5,7},{7,5}} | collective-permute-start | bytes 589832 | tf_op jit(solution)/shard_map/ppermute | solution.py:405
  468.3 169.8 %collective-permute-start.21 = (bf16[128,768]{1,0:T(8,128)(2,1)S(1)}, bf16[128,768]{1,0:T(8,128)(2,1)S(1)}, u32[]{:S(2)}, u32[]{:S(2)}) collective-permute-start(bf16[128,768]{1,0:T(8,128)(2,1)S(1)} %get-tuple-element.196.refs_1_), channel_id=1, source_target_pairs={{0,4},{4,0},{1,5},{5,1},{2,6},{6,2},{3,7},{7,3}} | collective-permute-start | bytes 589832 | tf_op jit(solution)/shard_map/ppermute | solution.py:405
  622.8 13.3 collective-permute-start.29
  641.1 7.9 collective-permute-start.41
  644.8 13.3 collective-permute-start.25
  644.8 13.3 collective-permute-start.24
  649.0 10.6 collective-permute-start.33
  649.0 12.0 collective-permute-start.30
  658.1 22.3 %collective-permute-start.31 = (bf16[128,768]{1,0:T(8,128)(2,1)S(1)}, bf16[128,768]{1,0:T(8,128)(2,1)S(1)}, u32[]{:S(2)}, u32[]{:S(2)}) collective-permute-start(bf16[128,768]{1,0:T(8,128)(2,1)S(1)} %get-tuple-element.179.refs_1_), channel_id=1, source_target_pairs={{0,4},{4,0},{1,5},{5,1},{2,6},{6,2},{3,7},{7,3}} | collective-permute-start | bytes 589832 | tf_op jit(solution)/shard_map/ppermute | solution.py:405
  658.1 22.3 %collective-permute-start.32 = (bf16[128,768]{1,0:T(8,128)(2,1)S(1)}, bf16[128,768]{1,0:T(8,128)(2,1)S(1)}, u32[]{:S(2)}, u32[]{:S(2)}) collective-permute-start(bf16[128,768]{1,0:T(8,128)(2,1)S(1)} %get-tuple-element.180.refs_0_), channel_id=1, source_target_pairs={{0,2},{2,0},{1,3},{3,1},{4,6},{6,4},{5,7},{7,5}} | collective-permute-start | bytes 589832 | tf_op jit(solution)/shard_map/ppermute | solution.py:405
  659.6 22.3 %collective-permute-start.35 = (bf16[128,768]{1,0:T(8,128)(2,1)S(1)}, bf16[128,768]{1,0:T(8,128)(2,1)S(1)}, u32[]{:S(2)}, u32[]{:S(2)}) collective-permute-start(bf16[128,768]{1,0:T(8,128)(2,1)S(1)} %collective-permute-done.33.refs_5_), channel_id=1, source_target_pairs={{0,4},{4,0},{1,5},{5,1},{2,6},{6,2},{3,7},{7,3}} | collective-permute-start | bytes 589832 | tf_op jit(solution)/shard_map/ppermute | solution.py:405
  661.0 22.4 %collective-permute-start.34 = (bf16[128,768]{1,0:T(8,128)(2,1)S(1)}, bf16[128,768]{1,0:T(8,128)(2,1)S(1)}, u32[]{:S(2)}, u32[]{:S(2)}) collective-permute-start(bf16[128,768]{1,0:T(8,128)(2,1)S(1)} %collective-permute-done.30.refs_2_), channel_id=1, source_target_pairs={{0,2},{2,0},{1,3},{3,1},{4,6},{6,4},{5,7},{7,5}} | collective-permute-start | bytes 589832 | tf_op jit(solution)/shard_map/ppermute | solution.py:405
  680.4 34.8 %collective-permute-start.42 = (bf16[128,768]{1,0:T(8,128)(2,1)S(1)}, bf16[128,768]{1,0:T(8,128)(2,1)S(1)}, u32[]{:S(2)}, u32[]{:S(2)}) collective-permute-start(bf16[128,768]{1,0:T(8,128)(2,1)S(1)} %get-tuple-element.183.refs_1_), channel_id=1, source_target_pairs={{0,4},{4,0},{1,5},{5,1},{2,6},{6,2},{3,7},{7,3}} | collective-permute-start | bytes 589832 | tf_op jit(solution)/shard_map/ppermute | solution.py:405
  680.5 34.8 %collective-permute-start.43 = (bf16[128,768]{1,0:T(8,128)(2,1)S(1)}, bf16[128,768]{1,0:T(8,128)(2,1)S(1)}, u32[]{:S(2)}, u32[]{:S(2)}) collective-permute-start(bf16[128,768]{1,0:T(8,128)(2,1)S(1)} %get-tuple-element.184.refs_0_), channel_id=1, source_target_pairs={{0,2},{2,0},{1,3},{3,1},{4,6},{6,4},{5,7},{7,5}} | collective-permute-start | bytes 589832 | tf_op jit(solution)/shard_map/ppermute | solution.py:405
  681.9 35.5 %collective-permute-start.46 = (bf16[128,768]{1,0:T(8,128)(2,1)S(1)}, bf16[128,768]{1,0:T(8,128)(2,1)S(1)}, u32[]{:S(2)}, u32[]{:S(2)}) collective-permute-start(bf16[128,768]{1,0:T(8,128)(2,1)S(1)} %collective-permute-done.44.refs_5_), channel_id=1, source_target_pairs={{0,4},{4,0},{1,5},{5,1},{2,6},{6,2},{3,7},{7,3}} | collective-permute-start | bytes 589832 | tf_op jit(solution)/shard_map/ppermute | solution.py:405
  683.4 34.0 %collective-permute-start.45 = (bf16[128,768]{1,0:T(8,128)(2,1)S(1)}, bf16[128,768]{1,0:T(8,128)(2,1)S(1)}, u32[]{:S(2)}, u32[]{:S(2)}) collective-permute-start(bf16[128,768]{1,0:T(8,128)(2,1)S(1)} %collective-permute-done.41.refs_2_), channel_id=1, source_target_pairs={{0,2},{2,0},{1,3},{3,1},{4,6},{6,4},{5,7},{7,5}} | collective-permute-start | bytes 589832 | tf_op jit(solution)/shard_map/ppermute | solution.py:405
  705.4 10.6 collective-permute-start.49
  715.2 24.1 %collective-permute-start.47 = (bf16[128,768]{1,0:T(8,128)(2,1)S(1)}, bf16[128,768]{1,0:T(8,128)(2,1)S(1)}, u32[]{:S(2)}, u32[]{:S(2)}) collective-permute-start(bf16[128,768]{1,0:T(8,128)(2,1)S(1)} %copy-done.33), channel_id=1, source_target_pairs={{0,4},{4,0},{1,5},{5,1},{2,6},{6,2},{3,7},{7,3}} | collective-permute-start | bytes 589832 | tf_op jit(solution)/shard_map/ppermute | solution.py:405
  715.3 24.1 %collective-permute-start.48 = (bf16[128,768]{1,0:T(8,128)(2,1)S(1)}, bf16[128,768]{1,0:T(8,128)(2,1)S(1)}, u32[]{:S(2)}, u32[]{:S(2)}) collective-permute-start(bf16[128,768]{1,0:T(8,128)(2,1)S(1)} %copy-done.35), channel_id=1, source_target_pairs={{0,2},{2,0},{1,3},{3,1},{4,6},{6,4},{5,7},{7,5}} | collective-permute-start | bytes 589832 | tf_op jit(solution)/shard_map/ppermute | solution.py:405
  716.0 23.4 %collective-permute-start.50 = (bf16[128,768]{1,0:T(8,128)(2,1)S(1)}, bf16[128,768]{1,0:T(8,128)(2,1)S(1)}, u32[]{:S(2)}, u32[]{:S(2)}) collective-permute-start(bf16[128,768]{1,0:T(8,128)(2,1)S(1)} %collective-permute-done.49.refs_5_), channel_id=1, source_target_pairs={{0,4},{4,0},{1,5},{5,1},{2,6},{6,2},{3,7},{7,3}} | collective-permute-start | bytes 589832 | tf_op jit(solution)/shard_map/ppermute | solution.py:405
  761.9 20.2 %collective-permute-start.51 = (f32[384,4096]{1,0:T(8,128)}, f32[384,4096]{1,0:T(8,128)S(1)}, u32[]{:S(2)}, u32[]{:S(2)}) collective-permute-start(f32[384,4096]{1,0:T(8,128)} %get-tuple-element.119), channel_id=1, source_target_pairs={{0,1},{1,0},{2,3},{3,2},{4,5},{5,4},{6,7},{7,6}} | collective-permute-start | bytes 18874376 | tf_op jit(solution)/shard_map/ppermute | solution.py:405
  767.3 9.6 collective-permute-start.52
  788.1 15.5 collective-permute-start.55
  1003.9 19.4 %collective-permute-start.59 = (f32[384,4096]{1,0:T(8,128)}, f32[384,4096]{1,0:T(8,128)}, u32[]{:S(2)}, u32[]{:S(2)}) collective-permute-start(f32[384,4096]{1,0:T(8,128)} %get-tuple-element.122), channel_id=1, source_target_pairs={{0,1},{1,0},{2,3},{3,2},{4,5},{5,4},{6,7},{7,6}} | collective-permute-start | bytes 18874376 | tf_op jit(solution)/shard_map/ppermute | solution.py:405
  1009.9 8.4 collective-permute-start.60
  1035.6 13.5 collective-permute-start.63
  1250.7 19.6 %collective-permute-start.67 = (f32[384,4096]{1,0:T(8,128)}, f32[384,4096]{1,0:T(8,128)}, u32[]{:S(2)}, u32[]{:S(2)}) collective-permute-start(f32[384,4096]{1,0:T(8,128)} %get-tuple-element.127), channel_id=1, source_target_pairs={{0,1},{1,0},{2,3},{3,2},{4,5},{5,4},{6,7},{7,6}} | collective-permute-start | bytes 18874376 | tf_op jit(solution)/shard_map/ppermute | solution.py:405
  1256.9 8.4 collective-permute-start.68
  1282.4 13.5 collective-permute-start.71
  1500.7 36.6 %collective-permute-start.75 = (f32[4,2,128,768]{3,2,1,0:T(8,128)S(1)}, f32[4,2,128,768]{3,2,1,0:T(8,128)}, u32[]{:S(2)}, u32[]{:S(2)}) collective-permute-start(f32[4,2,128,768]{3,2,1,0:T(8,128)S(1)} %maximum_select_fusion.5), channel_id=1, source_target_pairs={{4,0},{6,2},{1,5},{3,7}} | collective-permute-start | bytes 9437192 | tf_op jit(solution)/shard_map/ppermute | solution.py:534
  1504.8 105.6 %collective-permute-start.79 = (f32[384,4096]{1,0:T(8,128)}, f32[384,4096]{1,0:T(8,128)}, u32[]{:S(2)}, u32[]{:S(2)}) collective-permute-start(f32[384,4096]{1,0:T(8,128)} %get-tuple-element.132), channel_id=1, source_target_pairs={{0,1},{1,0},{2,3},{3,2},{4,5},{5,4},{6,7},{7,6}} | collective-permute-start | bytes 18874376 | tf_op jit(solution)/shard_map/ppermute | solution.py:405
  1506.8 80.3 %collective-permute-start.76 = (f32[4,2,128,768]{3,2,1,0:T(8,128)S(1)}, f32[4,2,128,768]{3,2,1,0:T(8,128)}, u32[]{:S(2)}, u32[]{:S(2)}) collective-permute-start(f32[4,2,128,768]{3,2,1,0:T(8,128)S(1)} %maximum_select_fusion.5), channel_id=1, source_target_pairs={{0,2},{2,0},{5,7},{7,5}} | collective-permute-start | bytes 9437192 | tf_op jit(solution)/shard_map/ppermute | solution.py:535
  1537.3 49.9 %collective-permute-start.77 = (f32[4,2,128,768]{3,2,1,0:T(8,128)}, f32[4,2,128,768]{3,2,1,0:T(8,128)}, u32[]{:S(2)}, u32[]{:S(2)}) collective-permute-start(f32[4,2,128,768]{3,2,1,0:T(8,128)} %collective-permute-done.75), channel_id=1, source_target_pairs={{0,2},{2,0},{5,7},{7,5}} | collective-permute-start | bytes 9437192 | tf_op jit(solution)/shard_map/ppermute | solution.py:536
  1539.7 8.5 collective-permute-start.80
  1551.1 32.5 %collective-permute-start.82 = (f32[768]{0:T(1024)S(1)}, f32[768]{0:T(1024)S(1)}, u32[]{:S(2)}, u32[]{:S(2)}) collective-permute-start(f32[768]{0:T(1024)S(1)} %add.489), channel_id=1, source_target_pairs={{0,4},{4,0},{1,5},{5,1},{2,6},{6,2},{3,7},{7,3}} | collective-permute-start | bytes 9224 | tf_op jit(solution)/shard_map/ppermute | solution.py:405
  1609.1 165.1 %collective-permute-start.78 = (f32[4096,768]{1,0:T(8,128)}, f32[4096,768]{1,0:T(8,128)}, u32[]{:S(2)}, u32[]{:S(2)}) collective-permute-start(f32[4096,768]{1,0:T(8,128)} %bitcast.131), channel_id=1, source_target_pairs={{0,1},{2,3},{5,4},{7,6}} | collective-permute-start | bytes 37748744 | tf_op jit(solution)/shard_map/ppermute | solution.py:540
  1620.0 144.0 %collective-permute-start.83 = (f32[384,4096]{1,0:T(8,128)}, f32[384,4096]{1,0:T(8,128)}, u32[]{:S(2)}, u32[]{:S(2)}) collective-permute-start(f32[384,4096]{1,0:T(8,128)} %multiply_divide_fusion), channel_id=1, source_target_pairs={{0,4},{4,0},{1,5},{5,1},{2,6},{6,2},{3,7},{7,3}} | collective-permute-start | bytes 18874376 | tf_op jit(solution)/shard_map/ppermute | solution.py:405
  1772.9 15.4 collective-permute-start.84
  (91 other events, 1842.9 us)

commit v2 on v0

v2 whole, which is shorter than its diff:
```python
import functools

import jax
import jax.numpy as jnp
from jax import lax
from jax.experimental import pallas as pl
from jax.experimental.pallas import tpu as pltpu
from jax.sharding import Mesh, PartitionSpec as P

SWEEPS = 4
EPS = 1e-6
F32 = jnp.float32
BF16 = jnp.bfloat16
MIB = 2 ** 20
ALL = ('y', 'x', 'c')
MESH = pl.DeviceIdType.MESH
CONTRACT_WORDS = (((1,), (1,)), ((), ()))
CONTRACT_DOCS = (((0,), (0,)), ((), ()))


def ratio(c_tile, z_tile):
    return (c_tile.astype(F32) / (z_tile + EPS)).astype(BF16)


RS1A, RS1B, RS2A, RS2B, AY, AX, BX, BY, AF, BF, TR = range(11)
BLOCKS = 16


def sweep_kernel(first, tile, *refs):
    if first:
        c_own, w_ref, h1_ref, wsh_ref, sh_ref = refs[:5]
        keep_ref, send_ref, shard_ref, wout_ref, wsum_ref, c_rcv, h2_ref = refs[5:12]
        refs = refs[12:]
    else:
        c_own, c_rcv, w_ref, h1_ref, h2_ref, wsh_ref, sh_ref = refs[:7]
        keep_ref, send_ref, shard_ref, wout_ref, wsum_ref = refs[7:12]
        refs = refs[12:]
    cbuf, wbuf, hbuf, acc, sa, ka, sb, kb, ra, rb, r2a, r2b, wnew, csem, wsem, hsem, osem, ssem, rsem = refs[:19]
    if first:
        tr, cssem, crsem, hrsem = refs[19:]
    j, x, k = (lax.axis_index(axis) for axis in ALL)
    place = {'y': j, 'x': x, 'c': k}
    diag = j == k
    own, words = keep_ref.shape
    second = 'c' if first else 'y'
    v_pos = place[second]

    def flipped(axes):
        return {axis: 1 - place[axis] for axis in axes}

    barrier = pltpu.get_barrier_semaphore()
    greet = (('x',), ('y',), ('c',), ('y', 'c')) if first else (('x',), ('y',))
    for axes in greet:
        pl.semaphore_signal(barrier, inc=1, device_id=flipped(axes), device_id_type=MESH)
    pl.semaphore_wait(barrier, len(greet))

    def remote(src, dst, send, recv, axes):
        return pltpu.make_async_remote_copy(src_ref=src, dst_ref=dst, send_sem=send, recv_sem=recv,
                                            device_id=flipped(axes), device_id_type=MESH)

    def rows_of(chunk, u, v, colour):
        return pl.ds(pl.multiple_of(chunk * 1024 + (2 * u + v) * 256 + colour * 128, 128), 128)

    def copy_of(event, chunk):
        sems = ssem.at[chunk, event], rsem.at[chunk, event]
        pos = lax.rem(chunk, 2)
        if event == RS1A:
            return remote(sa.at[pos], ra.at[chunk], *sems, 'x')
        if event == RS1B:
            return remote(sb.at[pos], rb.at[chunk], *sems, second)
        if event == RS2A:
            return remote(ka.at[chunk, 0], r2a.at[chunk], *sems, second)
        if event == RS2B:
            return remote(kb.at[chunk, 0], r2b.at[chunk], *sems, 'x')
        if event == TR:
            return remote(ra.at[chunk], tr.at[chunk], *sems, 'yc')
        rows = {AY: (x, j, 0), AX: (x, j, 0), BX: (x, j, 1), BY: (x, j, 1), AF: (x, 1 - j, 0), BF: (1 - x, j, 1)}
        part = wnew.at[rows_of(chunk, *rows[event])]
        return remote(part, part, *sems, 'y' if event in (AY, BY, BF) else 'x')

    def first_sums(chunk):
        copy_of(RS1A, chunk).wait_recv()
        ka[chunk] += ra[chunk]
        copy_of(RS2A, chunk).start()
        copy_of(RS1B, chunk).wait_recv()
        kb[chunk] += rb[chunk]
        copy_of(RS2B, chunk).start()

    def publish_a(chunk, new):
        shard_ref[chunk, 0] = new
        wnew[rows_of(chunk, x, j, 0), :] = new.astype(BF16)
        copy_of(AY, chunk).start()
        copy_of(AX, chunk).start()
        wsum_ref[...] += jnp.sum(new, axis=0, keepdims=True)

    def publish_b(chunk, new):
        shard_ref[chunk, 1] = new
        wnew[rows_of(chunk, x, j, 1), :] = new.astype(BF16)
        copy_of(BX, chunk).start()
        copy_of(BY, chunk).start()
        wsum_ref[...] += jnp.sum(new, axis=0, keepdims=True)

    def update(chunk):
        copy_of(RS2A, chunk).wait_recv()
        new = wsh_ref[chunk, 0] * (ka[chunk, 1] + r2a[chunk]) / sh_ref[...]
        if first:
            ra[chunk, 0] = new
        else:
            publish_a(chunk, new)
        copy_of(RS2B, chunk).wait_recv()
        new = wsh_ref[chunk, 1] * (kb[chunk, 1] + r2b[chunk]) / sh_ref[...]
        if first:
            ra[chunk, 1] = new

            @pl.when(jnp.logical_not(diag))
            def _():
                copy_of(TR, chunk).start()
        else:
            publish_b(chunk, new)

    def settle(chunk):
        def turned(ref, colour):
            value = ref[chunk, colour]
            return jnp.where(k == 0, value, jnp.concatenate([value[:, own:], value[:, :own]], axis=1))

        @pl.when(diag)
        def _():
            publish_a(chunk, turned(ra, 0))
            publish_b(chunk, turned(ra, 1))

        @pl.when(jnp.logical_not(diag))
        def _():
            copy_of(TR, chunk).wait_recv()
            publish_a(chunk, turned(tr, 0))
            publish_b(chunk, turned(tr, 1))

    def forward(chunk):
        copy_of(AY, chunk).wait_recv()
        copy_of(AF, chunk).start()
        copy_of(BX, chunk).wait_recv()
        copy_of(BF, chunk).start()

    def arrived(chunk):
        for event in (AX, BY, AF, BF):
            copy_of(event, chunk).wait_recv()

    def trade_of(block):
        rows = pl.ds(pl.multiple_of(block * 256, 256), 256)
        return remote(c_own.at[rows], c_rcv.at[rows], cssem.at[block], crsem.at[block], 'yc')

    def trade_start(block):
        @pl.when(jnp.logical_not(diag))
        def _():
            trade_of(block).start()

    def h_trade():
        return remote(h1_ref, h2_ref, hrsem.at[0], hrsem.at[1], 'c')

    def quarter_of(step):
        u = jnp.where(step < 2, 1 - x, x)
        v = jnp.where(step % 2 == 0, 1 - v_pos, v_pos)
        return 2 * u + v

    def c_copy(ref, row, slot):
        return pltpu.make_async_copy(ref.at[pl.ds(row, 256)], cbuf.at[slot], csem.at[slot])

    def fetch_c(row, slot, products):
        if first and products:
            c_copy(c_own, row, slot).start()
            return

        @pl.when(diag)
        def _():
            c_copy(c_own, row, slot).start()

        @pl.when(jnp.logical_not(diag))
        def _():
            if first:
                trade_of(row // 256).wait_recv()
            c_copy(c_rcv, row, slot).start()

    def w_copy(row, slot):
        return pltpu.make_async_copy(w_ref.at[pl.ds(row, 256)], wbuf.at[slot], wsem.at[slot])

    def fetch_w_unit(unit, slot):
        row = pl.multiple_of((unit // 4) * 1024 + quarter_of(lax.rem(unit, 4)) * 256, 256)
        fetch_c(row, slot, True)
        w_copy(row, slot).start()

    def h_copies(own_ref, sib_ref, own_row, sib_row):
        return [pltpu.make_async_copy(ref.at[pl.ds(pl.multiple_of(row, own), own)], hbuf.at[pl.ds(n * own, own)],
                                      hsem.at[n])
                for n, (ref, row) in enumerate(((own_ref, own_row), (sib_ref, sib_row)))]

    if first:
        trade_start(0)
        trade_start(1)

        @pl.when(diag)
        def _():
            h_trade().start()
        loads = h_copies(h1_ref, h1_ref, 0, own)
    else:
        loads = h_copies(h1_ref, h2_ref, 0, 0)
    for load in loads:
        load.start()
    fetch_w_unit(jnp.int32(0), 0)
    for ref in (wsum_ref, keep_ref, send_ref):
        ref[...] = jnp.zeros_like(ref)
    for load in loads:
        load.wait()

    def w_unit(unit, carry):
        chunk, step = unit // 4, lax.rem(unit, 4)
        slot = lax.rem(unit, 2)

        @pl.when(unit < BLOCKS - 1)
        def _():
            fetch_w_unit(unit + 1, 1 - slot)

        c_copy(c_own, 0, slot).wait()
        w_copy(0, slot).wait()
        for t in range(words // tile):
            cols = pl.ds(t * tile, tile)
            h = hbuf[:, cols]
            z = jnp.dot(wbuf[slot], h, preferred_element_type=F32)
            q = ratio(cbuf[slot, :, cols], z)
            part = lax.dot_general(q, h, CONTRACT_WORDS, preferred_element_type=F32)
            if t == 0:
                acc[...] = part
            else:
                acc[...] += part

        @pl.when((chunk >= 2) & (step == 0))
        def _():
            copy_of(RS1A, chunk - 2).wait_send()
            copy_of(RS1B, chunk - 2).wait_send()

        pos = lax.rem(chunk, 2)

        @pl.when(step < 2)
        def _():
            sa[pos, step] = acc[:128]

        @pl.when(step >= 2)
        def _():
            ka[chunk, step - 2] = acc[:128]

        @pl.when(step % 2 == 0)
        def _():
            sb[pos, step // 2] = acc[128:]

        @pl.when(step % 2 == 1)
        def _():
            kb[chunk, step // 2] = acc[128:]

        @pl.when(step == 1)
        def _():
            copy_of(RS1A, chunk).start()

        @pl.when(step == 2)
        def _():
            copy_of(RS1B, chunk).start()

        if first:
            @pl.when(lax.rem(unit, 3) == 2)
            def _():
                trade_start(2 + unit // 3)

        @pl.when((step == 3) & (chunk >= 1))
        def _():
            first_sums(chunk - 1)
        return carry

    lax.fori_loop(0, BLOCKS, w_unit, 0)
    if first:
        def next_loads(ref):
            return h_copies(ref, ref, k * own, (1 - k) * own)

        @pl.when(diag)
        def _():
            for load in next_loads(h1_ref):
                load.start()

        @pl.when(jnp.logical_not(diag))
        def _():
            h_trade().wait_recv()
            for load in next_loads(h2_ref):
                load.start()

        update(0)
        trade_start(7)
        first_sums(3)
        for chunk in range(1, 4):
            update(chunk)
            trade_start(7 + chunk)
        for chunk in range(4):
            settle(chunk)
            trade_start(11 + chunk)
        for chunk in range(4):
            forward(chunk)
            if chunk == 0:
                trade_start(15)
        for load in next_loads(h1_ref):
            load.wait()
    else:
        update(0)
        forward(0)
        first_sums(3)
        update(1)
        forward(1)
        update(2)
    fetch_c(0, 0, False)

    def h_unit(unit, carry):
        chunk = unit // 4
        slot = lax.rem(unit, 2)

        @pl.when(unit < BLOCKS - 1)
        def _():
            fetch_c(pl.multiple_of((unit + 1) * 256, 256), 1 - slot, False)

        @pl.when(lax.rem(unit, 4) == 0)
        def _():
            arrived(chunk)
            block = pl.ds(pl.multiple_of(chunk * 1024, 1024), 1024)
            pltpu.make_async_copy(wnew.at[block], wout_ref.at[block], osem.at[chunk]).start()

        c_copy(c_own, 0, slot).wait()
        w = wnew[pl.ds(pl.multiple_of(unit * 256, 256), 256), :]
        for t in range(words // tile):
            cols = pl.ds(t * tile, tile)
            z = jnp.dot(w, hbuf[:, cols], preferred_element_type=F32)
            q = ratio(cbuf[slot, :, cols], z)
            part = lax.dot_general(w, q, CONTRACT_DOCS, preferred_element_type=F32)
            keep_ref[:, cols] += part[:own]
            send_ref[:, cols] += part[own:]

        if not first:
            @pl.when(unit == 1)
            def _():
                update(3)

            @pl.when(unit == 3)
            def _():
                forward(2)

            @pl.when(unit == 5)
            def _():
                forward(3)
        return carry

    lax.fori_loop(0, BLOCKS, h_unit, 0)
    for chunk in range(4):
        block = pl.ds(chunk * 1024, 1024)
        pltpu.make_async_copy(wnew.at[block], wout_ref.at[block], osem.at[chunk]).wait()
        for event in range(10):
            if event > 1 or chunk > 1:
                copy_of(event, chunk).wait_send()
    if first:
        @pl.when(diag)
        def _():
            h_trade().wait_send()

        @pl.when(jnp.logical_not(diag))
        def _():
            for chunk in range(4):
                copy_of(TR, chunk).wait_send()
            for block in range(BLOCKS):
                trade_of(block).wait_send()


def fused_sweep(first, arrays, shards, s_h):
    docs, words, topics = 4096, 4096, shards.shape[-1]
    vmem, hbm = pl.BlockSpec(memory_space=pltpu.VMEM), pl.BlockSpec(memory_space=pl.ANY)
    acc = jax.ShapeDtypeStruct((topics // 2, words), F32)
    part = pltpu.VMEM((4, 2, 128, topics), F32)
    two = pltpu.VMEM((2, 2, 128, topics), F32)
    last = pltpu.VMEM((4, 128, topics), F32)
    dma = pltpu.SemaphoreType.DMA
    outs = (acc, acc, jax.ShapeDtypeStruct(shards.shape, F32), jax.ShapeDtypeStruct((docs, topics), BF16),
            jax.ShapeDtypeStruct((1, topics), F32))
    scratch = [
        pltpu.VMEM((2, 256, words), BF16),
        pltpu.VMEM((2, 256, topics), BF16),
        pltpu.VMEM((topics, words), BF16),
        pltpu.VMEM((256, topics), F32),
        two, part, two, part, part, part, last, last,
        pltpu.VMEM((docs, topics), BF16),
        dma((2,)), dma((2,)), dma((2,)), dma((4,)), dma((4, 11)), dma((4, 11)),
    ]
    out_specs = [vmem, vmem, vmem, hbm, vmem]
    if first:
        outs += (jax.ShapeDtypeStruct((docs, words), BF16), jax.ShapeDtypeStruct((topics, words), BF16))
        out_specs += [hbm, hbm]
        scratch += [part, dma((BLOCKS,)), dma((BLOCKS,)), dma((2,))]
    return pl.pallas_call(
        functools.partial(sweep_kernel, first, 1024),
        out_shape=outs,
        in_specs=[hbm] * len(arrays) + [vmem] * 2,
        out_specs=out_specs,
        scratch_shapes=scratch,
        cost_estimate=pl.CostEstimate(flops=8 * docs * words * topics, bytes_accessed=100 * MIB, transcendentals=0),
        compiler_params=pltpu.CompilerParams(collective_id=int(first), has_side_effects=True,
                                             vmem_limit_bytes=67043328),
        name='first_sweep' if first else 'fused_sweep',
    )(*arrays, shards, s_h)


def swap(arr, axis):
    return lax.ppermute(arr, axis, [(0, 1), (1, 0)])


def flip(arr, k, axis):
    half = arr.shape[axis] // 2
    return jnp.where(k == 0, arr, jnp.roll(arr, half, axis=axis))


def mesh_sum(vec):
    for axis in ('c', 'x', 'y'):
        vec = vec + swap(vec, axis)
    return vec


def local_sweeps(c_blk, w_loc, h_loc):
    j, x, k = (lax.axis_index(axis) for axis in ALL)
    diag = j == k
    docs, topics = w_loc.shape
    half = topics // 2
    dev = lambda jj, xx, kk: jj * 4 + xx * 2 + kk

    s_h = jnp.sum(h_loc, axis=1)
    s_h = s_h + swap(s_h, 'c')
    s_h = s_h + swap(s_h, 'x')
    h_bf = h_loc.astype(BF16)
    w_bf = w_loc.astype(BF16)
    shards = lax.dynamic_slice_in_dim(w_loc.reshape(4, 4, 2, 128, topics), 2 * x + k, 1, 1)[:, 0]
    wanted = lax.dynamic_slice_in_dim(h_loc, (1 - k) * half, half, 0)
    h_own = jnp.where(diag, lax.dynamic_slice_in_dim(h_loc, k * half, half, 0), swap(wanted, 'c'))

    for sweep in range(SWEEPS):
        if sweep == 0:
            keep, send, shards, w_bf, w_sum, c_rcv, unused = fused_sweep(True, (c_blk, w_bf, h_bf), shards, s_h[None])
        else:
            h_sum = jnp.sum(h_own, axis=1)
            h_sum = flip(jnp.concatenate([h_sum, jnp.zeros_like(h_sum)]), k, 0)
            s_h = flip(mesh_sum(h_sum), k, 0)
            keep, send, shards, w_bf, w_sum = fused_sweep(
                False, (c_blk, c_rcv, w_bf, h_bf_own, h_bf_sib), shards, s_h[None])
        s_w = flip(mesh_sum(flip(w_sum[0], k, 0)), k, 0)[:half]
        h_own = h_own * (keep + swap(send, 'c')) / s_w[:, None]
        if sweep < SWEEPS - 1:
            h_bf_own = h_own.astype(BF16)
            h_bf_sib = swap(h_bf_own, 'c')

    own = flip(shards, k, 3)
    into = [(dev(1 - a, b, a), dev(a, b, a)) for a in range(2) for b in range(2)]
    cross = [(dev(a, b, a), dev(a, 1 - b, a)) for a in range(2) for b in range(2)]
    aside = [(dev(a, b, a), dev(a, b, 1 - a)) for a in range(2) for b in range(2)]
    from_y = lax.ppermute(own, ALL, into)
    from_x = lax.ppermute(own, ALL, cross)
    from_xy = lax.ppermute(from_y, ALL, cross)
    near = jnp.where(j == 0, jnp.stack([own, from_y], 1), jnp.stack([from_y, own], 1))
    far = jnp.where(j == 0, jnp.stack([from_x, from_xy], 1), jnp.stack([from_xy, from_x], 1))
    w_half = jnp.where(x == 0, jnp.stack([near, far], 1), jnp.stack([far, near], 1)).reshape(docs, topics)
    w_out = jnp.where(diag, w_half, lax.ppermute(w_half, ALL, aside))

    from_y = swap(h_own, 'y')
    mine = jnp.where(diag, h_own, from_y)
    other = swap(jnp.where(diag, from_y, h_own), 'c')
    h_out = jnp.where(k == 0, jnp.concatenate([mine, other]), jnp.concatenate([other, mine]))
    return w_out, h_out


def solution(mesh):
    fine = Mesh(mesh.devices.reshape(2, 2, 2), ALL)
    spec_c = P('y', ('x', 'c'))
    spec_w = P('y', None)
    spec_h = P(None, ('x', 'c'))
    return jax.shard_map(local_sweeps, mesh=fine, in_specs=(spec_c, spec_w, spec_h), out_specs=(spec_w, spec_h), check_vma=False)
```

time: 2720 us -> 1510 us (0.56)
  waiting for transfers between devices: 1940 us -> 208 us
  Pallas kernels: 0 us -> 1060 us
  matrix products: 593 us -> 0 us
  starting transfers between devices: 0.33 us -> 83.8 us
  local copies, waits for them, and re-layouts: 1.83 us -> 47.5 us
  blocking collectives: 41.3 us -> 0 us
    psum x8 -> x0, waiting for transfers between devices: 1940 us -> none  [the longest x4 1120 us: local_sweeps(): lax.psum(lax.dot_general(w_bf, q_blk, CONTRACT_DOCS, preferred_element_ty...]
    pallas_call x0 -> x4, Pallas kernels: none -> 1060 us  [fused_sweep(): pl.pallas_call(functools.partial(sweep_kernel, first, 1024), out_shape=ou...]
    dot_general x16 -> x0, matrix products: 593 us -> none  [the longest x8 309 us: ratio_block(): z_blk = jnp.dot(w_bf, h_bf, preferred_element_type=jnp.float32)]
    ppermute x0 -> x37, waiting for transfers between devices: none -> 208 us  [the longest x33 208 us: swap(): return lax.ppermute(arr, axis, [(0, 1), (1, 0)])]
    ppermute x0 -> x37, starting transfers between devices: none -> 83.8 us  [the longest x33 73.6 us: swap(): return lax.ppermute(arr, axis, [(0, 1), (1, 0)])]
    reduce_sum x8 -> x4, other arithmetic: 105 us -> 36.2 us  [the longest x3 23.8 us: local_sweeps(): h_sum = jnp.sum(h_own, axis=1)]
    select_n x0 -> x21, other arithmetic: none -> 41.4 us  [the longest x1 10.6 us: local_sweeps(): w_out = jnp.where(diag, w_half, lax.ppermute(w_half, ALL, aside))]
    psum x8 -> x0, blocking collectives: 41.3 us -> none  [the longest x4 25.4 us: local_sweeps(): s_h = lax.psum(jnp.sum(h_loc, axis=1), 'col')]
  transfers between devices with their start and end apart: 8 -> 37, of which waited for: 8 -> 23; matrix products, arithmetic and copies ran while one was open for 0% -> 5% of each run, Pallas kernels for 0% -> 30%
where the time goes in v2:
time: 1510 us; the launch traced here: 1500 us
  Pallas kernels  1060 us (70%)
  waiting for transfers between devices  208 us (14%)
  other arithmetic  101 us (7%)
  starting transfers between devices  83.8 us (6%)
  local copies, waits for them, and re-layouts  47.5 us (3%)
    pallas_call x4, Pallas kernels, fused_sweep(): pl.pallas_call(functools.partial(sweep_kernel, first, 1024), out_shape=ou...  1060 us
    ppermute x33, waiting for transfers between devices, swap(): return lax.ppermute(arr, axis, [(0, 1), (1, 0)])  208 us
    ppermute x33, starting transfers between devices, swap(): return lax.ppermute(arr, axis, [(0, 1), (1, 0)])  73.6 us
  transfers between devices with their start and end apart: 37, of which 23 were waited for; matrix products, arithmetic and copies ran while one was open for 5% of the time, Pallas kernels for 30%

profile of v2, /device:TPU:1, one launch (start us, length us, event | category | flops | bytes accessed | tf_op | source)
XLA Modules:
  0.0 1502.1 jit_solution(9914990802828959177)
XLA Ops:
  0.6 12.4 fusion.6
  13.0 6.1 constant_dynamic-slice_fusion
  19.6 2.2 collective-permute-start.1
  21.9 3.8 dynamic-slice_bitcast_fusion.refs_3_
  25.7 7.9 convert_element_type.15.refs_1_
  34.2 456.7 %first_sweep.1 = (f32[384,4096]{1,0:T(8,128)}, f32[384,4096]{1,0:T(8,128)}, f32[4,2,128,768]{3,2,1,0:T(8,128)}, bf16[4096,768]{1,0:T(8,128)(2,1)}, f32[1,768]{1,...) custom-call(bf16[4096,4096]{1,0:T(8,128)(2,1)} %refs_0_.7, ...), custom_call_target="tpu_custom_call" | custom-call | flops 103079215104 | bytes 104857600 | tf_op jit(solution)/shard_map/first_sweep/pallas_call | solution.py:397
  490.9 37.8 %collective-permute-start.3 = (f32[384,4096]{1,0:T(8,128)}, f32[384,4096]{1,0:T(8,128)}, u32[]{:S(2)}, u32[]{:S(2)}) collective-permute-start(f32[384,4096]{1,0:T(8,128)} %get-tuple-element.25), channel_id=1, source_target_pairs={{0,1},{1,0},{2,3},{3,2},{4,5},{5,4},{6,7},{7,6}} | collective-permute-start | bytes 18874376 | tf_op jit(solution)/shard_map/ppermute | solution.py:411
  530.2 8.3 collective-permute-done.4
  541.3 2.1 collective-permute-done.6
  543.5 8.9 fusion.5
  552.4 2.7 copy-done
  555.6 1.7 copy-done.6
  558.2 5.3 collective-permute-done.8
  565.9 1.9 collective-permute-start.10
  569.4 1.7 copy-done.10
  571.1 202.1 %fused_sweep.3 = (f32[384,4096]{1,0:T(8,128)}, f32[384,4096]{1,0:T(8,128)}, f32[4,2,128,768]{3,2,1,0:T(8,128)}, bf16[4096,768]{1,0:T(8,128)(2,1)}, f32[1,768]{1,0:T(1,128)}) custom-call(bf16[4096,4096]{1,0:T(8,128)(2,1)} %refs_0_.7, bf16[4096,4096]{1,0:T(8,128)(2,1)} %get-tuple-element.22.refs_1_, bf16[4096,768]{1,0:T(8,128)(2,1)} %get-tuple-element.23.refs_2_, ...), custom_call_target="tpu_custom_call" | custom-call | flops 103079215104 | bytes 104857600 | tf_op jit(solution)/shard_map/fused_sweep/pallas_call | solution.py:397
  773.1 3.9 collective-permute-start.11
  778.5 8.3 collective-permute-done.12
  787.4 1.9 collective-permute-done.13
  789.9 1.9 collective-permute-done.14
  791.8 7.4 fusion.4
  799.2 2.7 copy-done.2
  802.4 1.7 copy-done.7
  804.1 2.7 collective-permute-start.15
  806.8 5.3 collective-permute-done.16
  812.6 1.9 collective-permute-done.17
  815.1 1.9 collective-permute-done.18
  817.6 1.6 copy-done.11
  819.2 200.9 %fused_sweep.4 = (f32[384,4096]{1,0:T(8,128)}, f32[384,4096]{1,0:T(8,128)}, f32[4,2,128,768]{3,2,1,0:T(8,128)}, bf16[4096,768]{1,0:T(8,128)(2,1)}, f32[1,768]{1,0:T(1,128)}) custom-call(bf16[4096,4096]{1,0:T(8,128)(2,1)} %refs_0_.7, bf16[4096,4096]{1,0:T(8,128)(2,1)} %get-tuple-element.22.refs_1_, bf16[4096,768]{1,0:T(8,128)(2,1)} %get-tuple-element.28.refs_2_, ...), custom_call_target="tpu_custom_call" | custom-call | flops 103079215104 | bytes 104857600 | tf_op jit(solution)/shard_map/fused_sweep/pallas_call | solution.py:397
  1020.1 3.9 collective-permute-start.19
  1025.5 8.3 collective-permute-done.20
  1034.4 1.9 collective-permute-done.21
  1036.9 1.9 collective-permute-done.22
  1038.8 7.4 fusion.3
  1046.2 2.7 copy-done.1
  1049.4 1.7 copy-done.5
  1051.0 2.7 collective-permute-start.23
  1053.8 5.3 collective-permute-done.24
  1059.6 1.9 collective-permute-done.25
  1062.1 1.9 collective-permute-done.26
  1064.6 1.6 copy-done.9
  1066.2 201.0 %fused_sweep.5 = (f32[384,4096]{1,0:T(8,128)}, f32[384,4096]{1,0:T(8,128)}, f32[4,2,128,768]{3,2,1,0:T(8,128)}, bf16[4096,768]{1,0:T(8,128)(2,1)}, f32[1,768]{1,0:T(1,128)}) custom-call(bf16[4096,4096]{1,0:T(8,128)(2,1)} %refs_0_.7, bf16[4096,4096]{1,0:T(8,128)(2,1)} %get-tuple-element.22.refs_1_, bf16[4096,768]{1,0:T(8,128)(2,1)} %get-tuple-element.33.refs_2_, ...), custom_call_target="tpu_custom_call" | custom-call | flops 103079215104 | bytes 104857600 | tf_op jit(solution)/shard_map/fused_sweep/pallas_call | solution.py:397
  1267.3 3.9 collective-permute-start.31
  1271.2 2.1 fusion.7
  1273.7 4.2 collective-permute-start.27
  1277.9 3.1 collective-permute-done.32
  1281.5 2.3 collective-permute-done.33
  1284.0 2.4 collective-permute-start.28
  1286.4 24.0 %collective-permute-done.34 = f32[768]{0:T(1024)S(1)} collective-permute-done((f32[768]{0:T(1024)S(1)}, f32[768]{0:T(1024)S(1)}, u32[]{:S(2)}, u32[]{:S(2)}) %collective-permute-start.34) | collective-permute-done | bytes 3104 | tf_op jit(solution)/shard_map/ppermute | solution.py:411
  1310.4 2.3 collective-permute-start.29
  1312.8 11.8 multiply_divide_fusion
  1324.5 2.4 collective-permute-start.35
  1326.9 3.6 maximum_select_fusion.2
  1330.5 5.9 maximum_select_fusion.3
  1336.5 5.1 maximum_select_fusion
  1341.6 10.7 copy.7
  1352.3 1.3 collective-permute-start.30
  1353.6 107.3 %collective-permute-done.35 = f32[384,4096]{1,0:T(8,128)} collective-permute-done((f32[384,4096]{1,0:T(8,128)}, f32[384,4096]{1,0:T(8,128)}, u32[]{:S(2)}, u32[]{:S(2)}) %collective-permute-start.35) | collective-permute-done | bytes 6291488 | tf_op jit(solution)/shard_map/ppermute | solution.py:411
  1460.9 8.9 broadcast_select_fusion.2
  1469.8 2.5 collective-permute-start.36
  1472.3 9.8 collective-permute-done.36
  1482.1 6.9 maximum_select_fusion.1
  1489.0 2.1 copy-done.3
  1491.1 10.6 broadcast_select_fusion
  (118 shorter events, 21.7 us)
Async XLA Ops:
  13.0 6.6 collective-permute-start
  19.1 524.3 %collective-permute-start.2 = (f32[384,4096]{1,0:T(8,128)}, f32[384,4096]{1,0:T(8,128)}, u32[]{:S(2)}, u32[]{:S(2)}) collective-permute-start(f32[384,4096]{1,0:T(8,128)} %constant_dynamic-slice_fusion), channel_id=1, source_target_pairs={{0,1},{1,0},{2,3},{3,2},{4,5},{5,4},{6,7},{7,6}} | collective-permute-start | bytes 18874376 | tf_op jit(solution)/shard_map/ppermute | solution.py:411
  19.6 13.9 collective-permute-start.1
  490.9 52.6 %collective-permute-start.3 = (f32[384,4096]{1,0:T(8,128)}, f32[384,4096]{1,0:T(8,128)}, u32[]{:S(2)}, u32[]{:S(2)}) collective-permute-start(f32[384,4096]{1,0:T(8,128)} %get-tuple-element.25), channel_id=1, source_target_pairs={{0,1},{1,0},{2,3},{3,2},{4,5},{5,4},{6,7},{7,6}} | collective-permute-start | bytes 18874376 | tf_op jit(solution)/shard_map/ppermute | solution.py:411
  530.1 8.4 collective-permute-start.4
  538.5 2.5 collective-permute-start.5
  541.0 2.5 collective-permute-start.6
  552.4 2.7 copy-start
  555.6 1.7 copy-start.6
  557.2 12.1 collective-permute-start.7
  558.1 5.3 collective-permute-start.8
  563.4 2.5 collective-permute-start.9
  565.9 2.9 collective-permute-start.10
  569.4 1.7 copy-start.10
  773.1 18.6 %collective-permute-start.11 = (f32[384,4096]{1,0:T(8,128)}, f32[384,4096]{1,0:T(8,128)}, u32[]{:S(2)}, u32[]{:S(2)}) collective-permute-start(f32[384,4096]{1,0:T(8,128)} %get-tuple-element.30), channel_id=1, source_target_pairs={{0,1},{1,0},{2,3},{3,2},{4,5},{5,4},{6,7},{7,6}} | collective-permute-start | bytes 18874376 | tf_op jit(solution)/shard_map/ppermute | solution.py:411
  778.4 8.4 collective-permute-start.12
  786.8 2.5 collective-permute-start.13
  789.3 2.5 collective-permute-start.14
  799.2 2.7 copy-start.2
  802.4 1.7 copy-start.7
  804.1 13.5 collective-permute-start.15
  806.7 5.3 collective-permute-start.16
  812.0 2.5 collective-permute-start.17
  814.5 2.5 collective-permute-start.18
  817.6 1.6 copy-start.11
  1020.1 18.6 %collective-permute-start.19 = (f32[384,4096]{1,0:T(8,128)}, f32[384,4096]{1,0:T(8,128)}, u32[]{:S(2)}, u32[]{:S(2)}) collective-permute-start(f32[384,4096]{1,0:T(8,128)} %get-tuple-element.35), channel_id=1, source_target_pairs={{0,1},{1,0},{2,3},{3,2},{4,5},{5,4},{6,7},{7,6}} | collective-permute-start | bytes 18874376 | tf_op jit(solution)/shard_map/ppermute | solution.py:411
  1025.4 8.4 collective-permute-start.20
  1033.8 2.5 collective-permute-start.21
  1036.3 2.5 collective-permute-start.22
  1046.2 2.7 copy-start.1
  1049.4 1.7 copy-start.5
  1051.0 13.5 collective-permute-start.23
  1053.7 5.3 collective-permute-start.24
  1059.0 2.5 collective-permute-start.25
  1061.5 2.5 collective-permute-start.26
  1064.6 1.6 copy-start.9
  1267.3 6.1 copy-start.4
  1267.3 45.5 %collective-permute-start.31 = (f32[384,4096]{1,0:T(8,128)}, f32[384,4096]{1,0:T(8,128)}, u32[]{:S(2)}, u32[]{:S(2)}) collective-permute-start(f32[384,4096]{1,0:T(8,128)} %get-tuple-element.40), channel_id=1, source_target_pairs={{0,1},{1,0},{2,3},{3,2},{4,5},{5,4},{6,7},{7,6}} | collective-permute-start | bytes 18874376 | tf_op jit(solution)/shard_map/ppermute | solution.py:411
  1273.3 4.5 copy-start.8
  1273.7 36.7 %collective-permute-start.27 = (f32[4,2,128,768]{3,2,1,0:T(8,128)S(1)}, f32[4,2,128,768]{3,2,1,0:T(8,128)}, u32[]{:S(2)}, u32[]{:S(2)}) collective-permute-start(f32[4,2,128,768]{3,2,1,0:T(8,128)S(1)} %maximum_select_fusion.4), channel_id=1, source_target_pairs={{4,0},{6,2},{1,5},{3,7}} | collective-permute-start | bytes 9437192 | tf_op jit(solution)/shard_map/ppermute | solution.py:460
  1277.9 3.1 collective-permute-start.32
  1281.0 2.9 collective-permute-start.33
  1283.9 26.5 %collective-permute-start.34 = (f32[768]{0:T(1024)S(1)}, f32[768]{0:T(1024)S(1)}, u32[]{:S(2)}, u32[]{:S(2)}) collective-permute-start(f32[768]{0:T(1024)S(1)} %add.134), channel_id=1, source_target_pairs={{0,4},{4,0},{1,5},{5,1},{2,6},{6,2},{3,7},{7,3}} | collective-permute-start | bytes 9224 | tf_op jit(solution)/shard_map/ppermute | solution.py:411
  1284.0 46.5 %collective-permute-start.28 = (f32[4,2,128,768]{3,2,1,0:T(8,128)S(1)}, f32[4,2,128,768]{3,2,1,0:T(8,128)}, u32[]{:S(2)}, u32[]{:S(2)}) collective-permute-start(f32[4,2,128,768]{3,2,1,0:T(8,128)S(1)} %maximum_select_fusion.4), channel_id=1, source_target_pairs={{0,2},{2,0},{5,7},{7,5}} | collective-permute-start | bytes 9437192 | tf_op jit(solution)/shard_map/ppermute | solution.py:461
  1310.4 20.1 %collective-permute-start.29 = (f32[4,2,128,768]{3,2,1,0:T(8,128)}, f32[4,2,128,768]{3,2,1,0:T(8,128)}, u32[]{:S(2)}, u32[]{:S(2)}) collective-permute-start(f32[4,2,128,768]{3,2,1,0:T(8,128)} %collective-permute-done.27), channel_id=1, source_target_pairs={{0,2},{2,0},{5,7},{7,5}} | collective-permute-start | bytes 9437192 | tf_op jit(solution)/shard_map/ppermute | solution.py:462
  1324.5 136.4 %collective-permute-start.35 = (f32[384,4096]{1,0:T(8,128)}, f32[384,4096]{1,0:T(8,128)}, u32[]{:S(2)}, u32[]{:S(2)}) collective-permute-start(f32[384,4096]{1,0:T(8,128)} %multiply_divide_fusion), channel_id=1, source_target_pairs={{0,4},{4,0},{1,5},{5,1},{2,6},{6,2},{3,7},{7,3}} | collective-permute-start | bytes 18874376 | tf_op jit(solution)/shard_map/ppermute | solution.py:411
  1352.3 136.7 %collective-permute-start.30 = (f32[4096,768]{1,0:T(8,128)}, f32[4096,768]{1,0:T(8,128)}, u32[]{:S(2)}, u32[]{:S(2)}) collective-permute-start(f32[4096,768]{1,0:T(8,128)} %bitcast.11), channel_id=1, source_target_pairs={{0,1},{2,3},{5,4},{7,6}} | collective-permute-start | bytes 37748744 | tf_op jit(solution)/shard_map/ppermute | solution.py:466
  1469.8 12.3 collective-permute-start.36
  1482.1 8.9 copy-start.3
